TPU v7x, 8 devices: a whole 2x2x1 slice. The times are simulated.
8 devices in a mesh: rep: 2 (over y, z), dp: 4 (over x, core).
Axes of the slice: x: 2, y: 2, z: 1, core: 2. Of those that a mesh axis runs over, the one named last changes fastest.
Arguments:
- g_w_gate: bfloat16 [8, 2, 1152, 4608], P(('rep', 'dp')), parts along dimension 0
- g_w_up: bfloat16 [8, 2, 1152, 4608], P(('rep', 'dp')), parts along dimension 0
- g_w_down: bfloat16 [8, 2, 4608, 1152], P(('rep', 'dp')), parts along dimension 0
- w_gate: bfloat16 [2, 1152, 4608], replicated
- w_up: bfloat16 [2, 1152, 4608], replicated
- w_down: bfloat16 [2, 4608, 1152], replicated
- m_w_gate: float32 [2, 1152, 4608], P(None, 'dp')
- m_w_up: float32 [2, 1152, 4608], P(None, 'dp')
- m_w_down: float32 [2, 4608, 1152], P(None, 'dp')
- v_w_gate: float32 [2, 1152, 4608], P(None, 'dp')
- v_w_up: float32 [2, 1152, 4608], P(None, 'dp')
- v_w_down: float32 [2, 4608, 1152], P(None, 'dp')
Outputs:
- output 1: bfloat16 [4, 1152, 4608], P('rep'), parts along dimension 0
- output 2: bfloat16 [4, 1152, 4608], P('rep'), parts along dimension 0
- output 3: bfloat16 [4, 4608, 1152], P('rep'), parts along dimension 0
- output 4: float32 [4, 1152, 4608], P('rep', 'dp'), parts along dimension 0
- output 5: float32 [4, 1152, 4608], P('rep', 'dp'), parts along dimension 0
- output 6: float32 [4, 4608, 1152], P('rep', 'dp'), parts along dimension 0
- output 7: float32 [4, 1152, 4608], P('rep', 'dp'), parts along dimension 0
- output 8: float32 [4, 1152, 4608], P('rep', 'dp'), parts along dimension 0
- output 9: float32 [4, 4608, 1152], P('rep', 'dp'), parts along dimension 0
There are 2 independent parts. A program takes and returns all parts, laid end to end along the dimension named above; an argument that names none is the same for every part.
All inputs are finite; a program needn't handle non-finite values.
Results may differ from a plain program's by a relative error of at most 0.022.
Values are sent between devices in bfloat16 or wider.
A program may use at most 2 GiB of HBM per device.

v0:
```python
import jax
import jax.numpy as jnp
from jax import lax
from jax.sharding import PartitionSpec as P


def adamw(w, m, v, g):
    m = 0.9 * m + 0.1 * g
    v = 0.95 * v + 0.05 * g * g
    step = m * lax.rsqrt(v + 1e-8) + 0.1 * w
    return (w - 0.02 * step).astype(jnp.bfloat16), m, v


def solution(mesh):
    def step(*arrays):
        terms, weights, m, v = (arrays[i : i + 3] for i in (0, 3, 6, 9))
        gradients = [lax.psum_scatter(t[0], "dp", scatter_dimension=1, tiled=True).astype(jnp.float32) for t in terms]
        me = lax.axis_index("dp")
        own = [lax.dynamic_slice_in_dim(w, me * one.shape[1], one.shape[1], 1).astype(jnp.float32) for w, one in zip(weights, m, strict=True)]
        new = [adamw(w, m, v, g) for w, m, v, g in zip(own, m, v, gradients, strict=True)]
        whole = [lax.all_gather(one[0], "dp", axis=1, tiled=True) for one in new]
        return (*whole, *(one[1] for one in new), *(one[2] for one in new))

    all_of, cut = P(None, None, None), P(None, "dp", None)
    return jax.shard_map(
        step,
        mesh=mesh,
        in_specs=(P(("rep", "dp"), None, None, None),) * 3 + (all_of,) * 3 + (cut,) * 6,
        out_specs=(P("rep", None, None),) * 3 + (P("rep", "dp", None),) * 6,
        check_vma=False,
    )
```

profile of v0, /device:TPU:0, one launch (start us, length us, event | category | flops | bytes accessed | tf_op | source)
XLA Modules:
  0.0 897.6 jit_solution(8387292413272980500)
XLA Ops:
  7.2 0.0 reduce-scatter.8.cloned.1.call-start
  7.2 0.7 reduce-scatter.8.cloned.1.call-update
  7.9 0.0 reduce-scatter.6.cloned.1.call-start
  8.0 0.7 reduce-scatter.6.cloned.1.call-update
  8.7 0.0 reduce-scatter.4.cloned.1.call-start
  8.7 0.7 reduce-scatter.4.cloned.1.call-update
  9.4 0.0 all-gather.8.cloned.1.call-start
  9.4 149.5 %reduce-scatter.8.cloned.1.call-done = bf16[2,1152,1152]{2,1,0:T(8,128)(2,1)} async-done(((bf16[2,4608,1152]{2,1,0:T(8,128)(2,1)}), bf16[2,1152,1152]{2,1,0:T(8,128)(2,1)}) %reduce-scatter.8.cloned.1.call-update) | async-done | bytes 5308432 | tf_op jit(solution)/shard_map/reduce_scatter | solution.py:17
  159.0 21.9 %fusion.10 = (bf16[2,1152,1152]{2,1,0:T(8,128)(2,1)}, f32[2,1152,1152]{2,1,0:T(8,128)}, f32[2,1152,1152]{2,1,0:T(8,128)}) fusion(bf16[2,4608,1152]{2,1,0:T(8,128)(2,1)} %param.17, s32[]{:T(128)S(6)} %select_n.8, bf16[2,1152,1152]{2,1,0:T(8,128)(2,1)} %reduce-scatter.8.cloned.1.call-done, f32[2,1152,1152]{2,1,0:T(8,128)} %param.23, f32[2,1152,1152]{2,1,0:T(8,128)} %param.20), kind=kLoop, calls=%fused_computation.22 | loop fusion | flops 42467328 | bytes 58392580 | tf_op jit(solution)/shard_map/convert_element_type | solution.py:11
  180.9 0.0 all-gather.8.cloned.1.call-update
  180.9 0.0 all-gather.6.cloned.1.call-start
  180.9 126.2 %reduce-scatter.6.cloned.1.call-done = bf16[2,288,4608]{2,1,0:T(8,128)(2,1)} async-done(((bf16[2,1152,4608]{2,1,0:T(8,128)(2,1)}), bf16[2,288,4608]{2,1,0:T(8,128)(2,1)}) %reduce-scatter.6.cloned.1.call-update) | async-done | bytes 5308432 | tf_op jit(solution)/shard_map/reduce_scatter | solution.py:17
  307.1 21.8 %fusion.6 = (bf16[2,288,4608]{2,1,0:T(8,128)(2,1)}, f32[2,288,4608]{2,1,0:T(8,128)}, f32[2,288,4608]{2,1,0:T(8,128)}) fusion(bf16[2,1152,4608]{2,1,0:T(8,128)(2,1)} %param.16, s32[]{:T(128)S(6)} %select_n.7, bf16[2,288,4608]{2,1,0:T(8,128)(2,1)} %reduce-scatter.6.cloned.1.call-done, f32[2,288,4608]{2,1,0:T(8,128)} %param.22, f32[2,288,4608]{2,1,0:T(8,128)} %param.19), kind=kLoop, calls=%fused_computation.18 | loop fusion | flops 42467328 | bytes 58392580 | tf_op jit(solution)/shard_map/convert_element_type | solution.py:11
  328.9 0.0 all-gather.6.cloned.1.call-update
  328.9 0.0 all-gather.4.cloned.1.call-start
  329.0 126.3 %reduce-scatter.4.cloned.1.call-done = bf16[2,288,4608]{2,1,0:T(8,128)(2,1)} async-done(((bf16[2,1152,4608]{2,1,0:T(8,128)(2,1)}), bf16[2,288,4608]{2,1,0:T(8,128)(2,1)}) %reduce-scatter.4.cloned.1.call-update) | async-done | bytes 5308432 | tf_op jit(solution)/shard_map/reduce_scatter | solution.py:17
  455.3 21.8 %fusion.2 = (bf16[2,288,4608]{2,1,0:T(8,128)(2,1)}, f32[2,288,4608]{2,1,0:T(8,128)}, f32[2,288,4608]{2,1,0:T(8,128)}) fusion(bf16[2,1152,4608]{2,1,0:T(8,128)(2,1)} %param.15, s32[]{:T(128)S(6)} %select_n.7, bf16[2,288,4608]{2,1,0:T(8,128)(2,1)} %reduce-scatter.4.cloned.1.call-done, f32[2,288,4608]{2,1,0:T(8,128)} %param.21, f32[2,288,4608]{2,1,0:T(8,128)} %param.18), kind=kLoop, calls=%fused_computation.14 | loop fusion | flops 42467328 | bytes 58392580 | tf_op jit(solution)/shard_map/convert_element_type | solution.py:11
  477.1 0.0 all-gather.4.cloned.1.call-update
  477.1 109.1 %all-gather.8.cloned.1.call-done = bf16[2,4608,1152]{2,1,0:T(8,128)(2,1)} async-done(((bf16[2,1152,1152]{2,1,0:T(8,128)(2,1)}), bf16[2,4608,1152]{2,1,0:T(8,128)(2,1)}) %all-gather.8.cloned.1.call-update) | async-done | bytes 21233680 | tf_op jit(solution)/shard_map/all_gather | solution.py:21
  586.2 131.0 %all-gather.6.cloned.1.call-done = bf16[2,1152,4608]{2,1,0:T(8,128)(2,1)} async-done(((bf16[2,288,4608]{2,1,0:T(8,128)(2,1)}), bf16[2,1152,4608]{2,1,0:T(8,128)(2,1)}) %all-gather.6.cloned.1.call-update) | async-done | bytes 21233680 | tf_op jit(solution)/shard_map/all_gather | solution.py:21
  717.2 131.0 %all-gather.4.cloned.1.call-done = bf16[2,1152,4608]{2,1,0:T(8,128)(2,1)} async-done(((bf16[2,288,4608]{2,1,0:T(8,128)(2,1)}), bf16[2,1152,4608]{2,1,0:T(8,128)(2,1)}) %all-gather.4.cloned.1.call-update) | async-done | bytes 21233680 | tf_op jit(solution)/shard_map/all_gather | solution.py:21
  848.1 0.0 copy-start
  848.1 0.0 slice-start
  848.1 0.0 slice-start.1
  848.1 0.0 slice-start.2
  848.1 21.0 %copy.24 = bf16[2,1152,4608]{2,1,0:T(8,128)(2,1)} copy(bf16[2,1152,4608]{2,1,0:T(8,128)(2,1)} %all-gather.4.cloned.1.call-done) | data formatting | bytes 42467328
  869.1 0.0 copy-done
  869.1 0.0 slice-start.3
  869.1 0.0 slice-start.4
  869.1 0.0 slice-start.5
  869.1 10.8 %copy.25 = bf16[2,1152,4608]{2,1,0:T(8,128)(2,1)} copy(bf16[2,1152,4608]{2,1,0:T(8,128)(2,1)S(1)} %copy-done) | data formatting | bytes 42467328
  879.9 0.0 slice-done
  879.9 0.0 slice-done.1
  879.9 0.0 slice-done.2
  879.9 2.0 slice-done.3
  881.9 1.2 slice-done.4
  883.1 0.0 slice-done.5
  883.1 7.6 copy.26
  (1 shorter events, 0.0 us)
Async XLA Ops:
  7.2 151.8 %reduce-scatter.8.cloned.1.call-start = ((), (), s32[]{:S(2)}) async-start(), calls=%async_computation.7 | async-start | bytes 26542080 | tf_op jit(solution)/shard_map/reduce_scatter | solution.py:17
  7.9 299.2 %reduce-scatter.6.cloned.1.call-start = ((), (), s32[]{:S(2)}) async-start(), calls=%async_computation.5 | async-start | bytes 26542080 | tf_op jit(solution)/shard_map/reduce_scatter | solution.py:17
  8.7 446.6 %reduce-scatter.4.cloned.1.call-start = ((), (), s32[]{:S(2)}) async-start(), calls=%async_computation.3 | async-start | bytes 26542080 | tf_op jit(solution)/shard_map/reduce_scatter | solution.py:17
  9.4 576.8 %all-gather.8.cloned.1.call-start = ((), (), s32[]{:S(2)}) async-start(), calls=%async_computation.8 | async-start | bytes 26542080 | tf_op jit(solution)/shard_map/all_gather | solution.py:21
  180.9 536.3 %all-gather.6.cloned.1.call-start = ((), (), s32[]{:S(2)}) async-start(), calls=%async_computation.6 | async-start | bytes 26542080 | tf_op jit(solution)/shard_map/all_gather | solution.py:21
  328.9 519.2 %all-gather.4.cloned.1.call-start = ((), (), s32[]{:S(2)}) async-start(), calls=%async_computation.4 | async-start | bytes 26542080 | tf_op jit(solution)/shard_map/all_gather | solution.py:21
  848.1 21.0 %copy-start = (bf16[2,1152,4608]{2,1,0:T(8,128)(2,1)S(1)}, bf16[2,1152,4608]{2,1,0:T(8,128)(2,1)}, u32[]{:S(2)}) copy-start(bf16[2,1152,4608]{2,1,0:T(8,128)(2,1)} %all-gather.6.cloned.1.call-done) | copy-start | bytes 63700996
  848.1 31.8 %slice-start = ((s8[21233664]{0:T(1024)(128)(4,1)}), s8[4194304]{0:T(1024)(128)(4,1)S(1)}, s32[]{:S(2)}) async-start(s8[21233664]{0:T(1024)(128)(4,1)} %bitcast.6), calls=%async_computation.9 | async-start | bytes 8388608
  848.1 31.8 %slice-start.1 = ((s8[21233664]{0:T(1024)(128)(4,1)}), s8[4194304]{0:T(1024)(128)(4,1)S(1)}, s32[]{:S(2)}) async-start(s8[21233664]{0:T(1024)(128)(4,1)} %bitcast.6), calls=%async_computation.10 | async-start | bytes 8388608
  848.1 31.8 %slice-start.2 = ((s8[21233664]{0:T(1024)(128)(4,1)}), s8[4194304]{0:T(1024)(128)(4,1)S(1)}, s32[]{:S(2)}) async-start(s8[21233664]{0:T(1024)(128)(4,1)} %bitcast.6), calls=%async_computation.11 | async-start | bytes 8388608
  869.1 12.8 %slice-start.3 = ((s8[21233664]{0:T(1024)(128)(4,1)}), s8[4194304]{0:T(1024)(128)(4,1)S(1)}, s32[]{:S(2)}) async-start(s8[21233664]{0:T(1024)(128)(4,1)} %bitcast.6), calls=%async_computation.12 | async-start | bytes 8388608
  869.1 14.0 %slice-start.4 = ((s8[21233664]{0:T(1024)(128)(4,1)}), s8[4194304]{0:T(1024)(128)(4,1)S(1)}, s32[]{:S(2)}) async-start(s8[21233664]{0:T(1024)(128)(4,1)} %bitcast.6), calls=%async_computation.13 | async-start | bytes 8388608
  869.1 14.0 %slice-start.5 = ((s8[21233664]{0:T(1024)(128)(4,1)}), s8[262144]{0:T(1024)(128)(4,1)S(1)}, s32[]{:S(2)}) async-start(s8[21233664]{0:T(1024)(128)(4,1)} %bitcast.6), calls=%async_computation.14 | async-start | bytes 524288
Sparse Core Ops, SparseCore 0:
  10.5 148.3 reduce-scatter.7
  161.5 145.5 reduce-scatter.5
  309.7 145.5 reduce-scatter.3
  457.2 128.9 all-gather.7
  588.2 128.9 all-gather.5
  719.1 128.9 all-gather.3
where the time goes:
time: 898 us
  waiting for transfers between devices  775 us (86%)
  other arithmetic  65.5 us (7%)
  local copies, waits for them, and re-layouts  42.6 us (5%)
  between operations  14.1 us (2%)
    reduce_scatter x3, waiting for transfers between devices, step(): lax.psum_scatter(t[0], 'dp', scatter_dimension=1, tiled=True)  402 us
    all_gather x3, waiting for transfers between devices, step(): whole = [lax.all_gather(one[0], 'dp', axis=1, tiled=True) for one in new]  371 us
    convert_element_type x3, other arithmetic, adamw(): return ((w - 0.02 * step).astype(jnp.bfloat16), m, v)  65.5 us
    unnamed x17, local copies, waits for them, and re-layouts  42.6 us
  transfers between devices with their start and end apart: 6, of which 6 were waited for; matrix products, arithmetic and copies ran while one was open for 7% of the time, Pallas kernels for 0%

commit v1 on v0

v1 whole, which is shorter than its diff:
```python
import jax
import jax.numpy as jnp
from jax import lax
from jax.experimental import pallas as pl
from jax.experimental.pallas import tpu as pltpu
from jax.sharding import PartitionSpec as P


MESH = pl.DeviceIdType.MESH
BF16, F32 = jnp.bfloat16, jnp.float32
ANY = pl.BlockSpec(memory_space=pl.ANY)
PER_LAYER = 6


PARTNER = [(i, i ^ 1) for i in range(4)]
ACROSS = [(i, i ^ 2) for i in range(4)]


def pair_sums(*refs):
    g = refs[0:3]
    across0 = refs[3]
    theirs = refs[4:7]
    sums = (None, *refs[7:9])
    mine, landed = refs[9:12], refs[12:15]
    in_send, in_recv, load, out_send, out_recv, store, own_send, own_recv = refs[15:]

    rep, me = lax.axis_index("rep"), lax.axis_index("dp")
    chip, core = me // 2, me % 2
    partner = chip * 2 + (1 - core)
    across = (1 - chip) * 2 + core
    diagonal = (1 - chip) * 2 + (1 - core)

    barrier = pltpu.get_barrier_semaphore()
    for other in (partner, across):
        pl.semaphore_signal(barrier, inc=1, device_id=(rep, other), device_id_type=MESH)
    pl.semaphore_wait(barrier, 2)

    def piece(w, owner, t):
        rows = mine[w].shape[1]
        return g[w].at[0, t // PER_LAYER, pl.ds((owner * PER_LAYER + t % PER_LAYER) * rows, rows)]

    def place(ref, w, t):
        rows = mine[w].shape[1]
        return ref.at[t // PER_LAYER, pl.ds((t % PER_LAYER) * rows, rows)]

    def to_partner(w, t):
        return pltpu.make_async_remote_copy(
            piece(w, diagonal, t), landed[w].at[t], in_send.at[w, t], in_recv.at[w, t], device_id=(rep, partner), device_id_type=MESH
        )

    def to_mine(w, t):
        return pltpu.make_async_copy(piece(w, across, t), mine[w].at[t], load.at[w, t])

    def send_across(t):
        return pltpu.make_async_remote_copy(
            mine[0].at[t], place(across0, 0, t), out_send.at[t], out_recv.at[t], device_id=(rep, across), device_id_type=MESH
        )

    def keep(w, t):
        return pltpu.make_async_copy(mine[w].at[t], place(sums[w], w, t), store.at[w - 1, t])

    def own_terms(w):
        rows = theirs[w].shape[1]
        return pltpu.make_async_remote_copy(
            g[w].at[0, :, pl.ds(partner * rows, rows)], theirs[w], own_send.at[w], own_recv.at[w], device_id=(rep, partner), device_id_type=MESH
        )

    def add(w, t):
        to_partner(w, t).wait_recv()
        to_mine(w, t).wait()
        mine[w][t] = (mine[w][t].astype(F32) + landed[w][t].astype(F32)).astype(BF16)

    pieces = 2 * PER_LAYER

    @pl.loop(0, pieces)
    def _(t):
        to_partner(0, t).start()
        to_mine(0, t).start()

    @pl.loop(0, pieces)
    def _(t):
        add(0, t)
        send_across(t).start()
        for w in (1, 2):
            to_partner(w, t).start()
            to_mine(w, t).start()

    for w in range(3):
        own_terms(w).start()

    for w in (1, 2):

        @pl.loop(0, pieces)
        def _(t, w=w):
            add(w, t)
            keep(w, t).start()

    @pl.loop(0, pieces)
    def _(t):
        for w in range(3):
            to_partner(w, t).wait_send()
        for w in (1, 2):
            keep(w, t).wait()

    for w in range(3):
        own_terms(w).wait()

    @pl.loop(0, pieces)
    def _(t):
        send_across(t).wait()


def exchange(terms, blocks):
    shapes = [(2, *b) for b in blocks]
    vmem = [pltpu.VMEM((2 * PER_LAYER, b[0] // PER_LAYER, b[1]), BF16) for b in blocks]
    pieces = 2 * PER_LAYER
    dma = pltpu.SemaphoreType.DMA
    return pl.pallas_call(
        pair_sums,
        out_shape=[jax.ShapeDtypeStruct(s, BF16) for s in (shapes[0], *shapes, *shapes[1:])],
        in_specs=[ANY] * 3,
        out_specs=[ANY] * 6,
        scratch_shapes=[
            *vmem,
            *vmem,
            dma((3, pieces)),
            dma((3, pieces)),
            dma((3, pieces)),
            dma((pieces,)),
            dma((pieces,)),
            dma((2, pieces)),
            dma((3,)),
            dma((3,)),
        ],
        compiler_params=pltpu.CompilerParams(collective_id=0, has_side_effects=True, vmem_limit_bytes=60 << 20),
        cost_estimate=pl.CostEstimate(flops=10**8, bytes_accessed=10**8, transcendentals=0),
        name="pair_sums",
    )(*terms)


def adamw(splits, where, g, theirs, arrived, m, v, w):
    layers, block, columns = m.shape
    rows = block // PER_LAYER
    steps = layers * PER_LAYER
    firsts = [first // rows for first, _ in splits]
    counts = [size // rows for _, size in splits]

    def body(where_ref, g_ref, theirs_ref, arrived_ref, m_ref, v_ref, w_ref, m_out, v_out, w_out, *parts):
        total = (g_ref[0, 0].astype(F32) + theirs_ref[0].astype(F32)) + arrived_ref[0].astype(F32)
        grad = total.astype(BF16).astype(F32)
        old = w_ref[0].astype(F32)
        new_m = 0.9 * m_ref[0] + 0.1 * grad
        new_v = 0.95 * v_ref[0] + 0.05 * grad * grad
        step = new_m * lax.rsqrt(new_v + 1e-8) + 0.1 * old
        new_w = (old - 0.02 * step).astype(BF16)
        m_out[0] = new_m
        v_out[0] = new_v
        w_out[0] = new_w
        i = pl.program_id(0)
        for part, first, count in zip(parts, firsts, counts, strict=True):

            @pl.when((i >= first) & (i < first + count))
            def _(part=part):
                part[...] = new_w

    def own(i, where):
        return (i // PER_LAYER, i % PER_LAYER, 0)

    def inside(i, where):
        return (i // PER_LAYER, where[0] * PER_LAYER + i % PER_LAYER, 0)

    def part_map(first, count):
        return lambda i, where: (jnp.clip(i - first, 0, count - 1), 0)

    tile = (1, rows, columns)
    return pl.pallas_call(
        body,
        grid_spec=pltpu.PrefetchScalarGridSpec(
            num_scalar_prefetch=1,
            grid=(steps,),
            in_specs=[
                pl.BlockSpec((1, *tile), lambda i, where: (0, *inside(i, where))),
                pl.BlockSpec(tile, own),
                pl.BlockSpec(tile, own),
                pl.BlockSpec(tile, own),
                pl.BlockSpec(tile, own),
                pl.BlockSpec(tile, inside),
            ],
            out_specs=[
                pl.BlockSpec(tile, own),
                pl.BlockSpec(tile, own),
                pl.BlockSpec(tile, inside),
                *(pl.BlockSpec((rows, columns), part_map(f, c)) for f, c in zip(firsts, counts, strict=True)),
            ],
        ),
        out_shape=[
            jax.ShapeDtypeStruct(m.shape, F32),
            jax.ShapeDtypeStruct(m.shape, F32),
            jax.ShapeDtypeStruct(w.shape, BF16),
            *(jax.ShapeDtypeStruct((size, columns), BF16) for _, size in splits),
        ],
        cost_estimate=pl.CostEstimate(flops=10**10, bytes_accessed=10**8, transcendentals=0),
        name="adamw",
    )(where, g, theirs, arrived, m, v, w)


def put(where, whole, after, block, first, arrived):
    columns = whole.shape[2]
    rows = block // PER_LAYER
    count = min(a.shape[0] for _, _, a in arrived) // rows
    n = len(arrived)

    def body(where_ref, *refs):
        out = refs[-1]
        j = pl.program_id(1)
        for k in range(n):

            @pl.when(j == k)
            def _(k=k):
                out[0] = refs[k][...]

    def in_map(skip):
        return lambda i, j, where: (i + skip // rows, 0)

    def out_map(i, j, where):
        t = i + first // rows
        owner = where[arrived[0][0]]
        for k in range(1, n):
            owner = jnp.where(j == k, where[arrived[k][0]], owner)
        return (t // PER_LAYER, owner * PER_LAYER + t % PER_LAYER, 0)

    return pl.pallas_call(
        body,
        grid_spec=pltpu.PrefetchScalarGridSpec(
            num_scalar_prefetch=1,
            grid=(count, n),
            in_specs=[*(pl.BlockSpec((rows, columns), in_map(skip)) for _, skip, _ in arrived), ANY, ANY],
            out_specs=pl.BlockSpec((1, rows, columns), out_map),
        ),
        out_shape=jax.ShapeDtypeStruct(whole.shape, BF16),
        input_output_aliases={n + 1: 0},
        compiler_params=pltpu.CompilerParams(vmem_limit_bytes=16 << 20),
        cost_estimate=pl.CostEstimate(flops=10**9, bytes_accessed=10**7, transcendentals=0),
        name="put",
    )(where, *(a for _, _, a in arrived), whole, after)


def send(array, pairs):
    return lax.ppermute(array, "dp", pairs)


def solution(mesh):
    def step(*arrays):
        terms, weights, ms, vs = (arrays[i : i + 3] for i in (0, 3, 6, 9))
        blocks = [m.shape[1:] for m in ms]
        where = lax.axis_index("dp") ^ jnp.arange(4, dtype=jnp.int32)
        across0, theirs0, theirs1, theirs2, sum1, sum2 = exchange(terms, blocks)
        arrived = [across0, send(sum1, ACROSS), send(sum2, ACROSS)]
        theirs = [theirs0, theirs1, theirs2]
        new_w, new_m, new_v = [], [], []
        after = where
        for k in range(3):
            block = blocks[k][0]
            rows = block // PER_LAYER
            splits = [(0, 2 * block)]
            if k == 2:
                sizes = (block, 4 * rows, rows, rows)
                splits += [(sum(sizes[:i]), sizes[i]) for i in range(4)]
            m, v, w, block_w, *parts = adamw(splits, where, terms[k], theirs[k], arrived[k], ms[k], vs[k], weights[k])
            parts = parts or [block_w]
            over = [send(a, ACROSS) for a in parts]
            beside = send(block_w, PARTNER)
            passed = [send(a, PARTNER) for a in over]
            first = 0
            for a, b in zip(over, passed, strict=True):
                w = put(where, w, after, block, first, [(1, first, beside), (2, 0, a), (3, 0, b)])
                first += a.shape[0]
            after = w
            new_w.append(w)
            new_m.append(m)
            new_v.append(v)
        return (*new_w, *new_m, *new_v)

    all_of, cut = P(None, None, None), P(None, "dp", None)
    return jax.shard_map(
        step,
        mesh=mesh,
        in_specs=(P(("rep", "dp"), None, None, None),) * 3 + (all_of,) * 3 + (cut,) * 6,
        out_specs=(P("rep", None, None),) * 3 + (P("rep", "dp", None),) * 6,
        check_vma=False,
    )
```

time: 898 us -> 789 us (0.88)
  waiting for transfers between devices: 775 us -> 475 us
  Pallas kernels: 0 us -> 286 us
  other arithmetic: 65.5 us -> 0.54 us
  local copies, waits for them, and re-layouts: 42.6 us -> 14.1 us
  between operations: 14.1 us -> 0.68 us
  starting transfers between devices: 0.24 us -> 11.8 us
    ppermute x0 -> x17, waiting for transfers between devices: none -> 475 us  [send(): return lax.ppermute(array, 'dp', pairs)]
    reduce_scatter x3 -> x0, waiting for transfers between devices: 402 us -> none  [step(): lax.psum_scatter(t[0], 'dp', scatter_dimension=1, tiled=True)]
    all_gather x3 -> x0, waiting for transfers between devices: 371 us -> none  [step(): whole = [lax.all_gather(one[0], 'dp', axis=1, tiled=True) for one in new]]
    pallas_call x0 -> x10, Pallas kernels: none -> 286 us  [the longest x1 122 us: exchange(): pl.pallas_call(pair_sums, out_shape=[jax.ShapeDtypeStruct(s, BF16) for s...]
    convert_element_type x3 -> x0, other arithmetic: 65.5 us -> none  [adamw(): return ((w - 0.02 * step).astype(jnp.bfloat16), m, v)]
    unnamed x17 -> x6, local copies, waits for them, and re-layouts: 42.6 us -> 14.1 us
    ppermute x0 -> x17, starting transfers between devices: none -> 11.8 us  [send(): return lax.ppermute(array, 'dp', pairs)]
  transfers between devices with their start and end apart: 6 -> 17, of which waited for: 6 -> 6; matrix products, arithmetic and copies ran while one was open for 7% -> 0% of each run, Pallas kernels for 0% -> 20%
where the time goes in v1:
time: 789 us; the launch traced here: 788 us
  waiting for transfers between devices  475 us (60%)
  Pallas kernels  286 us (36%)
  local copies, waits for them, and re-layouts  14.1 us (2%)
  starting transfers between devices  11.8 us (1%)
    ppermute x17, waiting for transfers between devices, send(): return lax.ppermute(array, 'dp', pairs)  475 us
    pallas_call x1, Pallas kernels, exchange(): pl.pallas_call(pair_sums, out_shape=[jax.ShapeDtypeStruct(s, BF16) for s...  122 us
    pallas_call x3, Pallas kernels, adamw(): pl.pallas_call(body, grid_spec=pltpu.PrefetchScalarGridSpec(num_scalar_pr...  88.7 us
    pallas_call x6, Pallas kernels, put(): pl.pallas_call(body, grid_spec=pltpu.PrefetchScalarGridSpec(num_scalar_pr...  75.2 us
  transfers between devices with their start and end apart: 17, of which 6 were waited for; matrix products, arithmetic and copies ran while one was open for 0% of the time, Pallas kernels for 20%

profile of v1, /device:TPU:0, one launch (start us, length us, event | category | flops | bytes accessed | tf_op | source)
XLA Modules:
  0.0 787.5 jit_solution(14091082016787914312)
XLA Ops:
  0.6 121.6 %pair_sums.1 = (bf16[2,288,4608]{2,1,0:T(8,128)(2,1)}, bf16[2,288,4608]{2,1,0:T(8,128)(2,1)}, bf16[2,288,4608]{2,1,0:T(8,128)(2,1)}, bf16[2,1152,1152]{2,1,0:T(8...) custom-call(bf16[1,2,1152,4608]{3,2,1,0:T(8,128)(2,1)} %g_ref.3, ...), custom_call_target="tpu_custom_call" | custom-call | flops 100000000 | bytes 100000000 | tf_op jit(solution)/shard_map/pair_sums/pallas_call | solution.py:118
  122.3 1.5 collective-permute-start.3
  123.8 0.6 collective-permute-start.7
  124.3 0.5 iota_xor_fusion.where_ref.refs_4_
  124.9 28.9 %adamw.3 = (f32[2,288,4608]{2,1,0:T(8,128)}, f32[2,288,4608]{2,1,0:T(8,128)}, bf16[2,1152,4608]{2,1,0:T(8,128)(2,1)}, bf16[576,4608]{1,0:T(8,128)(2,1)}) custom-call(s32[4]{0:T(128)} %iota_xor_fusion.where_ref.refs_4_, bf16[1,2,1152,4608]{3,2,1,0:T(8,128)(2,1)} %g_ref.3, bf16[2,288,4608]{2,1,0:T(8,128)(2,1)} %get-tuple-element.31.theirs_ref, ...), custom_call_target="tpu_custom_call" | custom-call | flops 10000000000 | bytes 100000000 | tf_op jit(solution)/shard_map/adamw/pallas_call | solution.py:176
  153.7 1.5 collective-permute-start.1
  155.2 0.0 collective-permute-start
  155.2 84.7 %collective-permute-done.3.arrived_ref = bf16[2,288,4608]{2,1,0:T(8,128)(2,1)} collective-permute-done((bf16[2,288,4608]{2,1,0:T(8,128)(2,1)}, bf16[2,288,4608]{2,1,0:T(8,128)(2,1)}, u32[]{:S(2)}, u32[]{:S(2)}) %collective-permute-start.3) | collective-permute-done | bytes 5308448 | tf_op jit(solution)/shard_map/ppermute | solution.py:249
  239.9 28.9 %adamw.4 = (f32[2,288,4608]{2,1,0:T(8,128)}, f32[2,288,4608]{2,1,0:T(8,128)}, bf16[2,1152,4608]{2,1,0:T(8,128)(2,1)}, bf16[576,4608]{1,0:T(8,128)(2,1)}) custom-call(s32[4]{0:T(128)} %iota_xor_fusion.where_ref.refs_4_, bf16[1,2,1152,4608]{3,2,1,0:T(8,128)(2,1)} %g_ref.4, bf16[2,288,4608]{2,1,0:T(8,128)(2,1)} %get-tuple-element.35.theirs_ref, ...), custom_call_target="tpu_custom_call" | custom-call | flops 10000000000 | bytes 100000000 | tf_op jit(solution)/shard_map/adamw/pallas_call | solution.py:176
  268.8 1.5 collective-permute-start.5
  270.3 83.4 %collective-permute-done.7.arrived_ref = bf16[2,1152,1152]{2,1,0:T(8,128)(2,1)} collective-permute-done((bf16[2,1152,1152]{2,1,0:T(8,128)(2,1)}, bf16[2,1152,1152]{2,1,0:T(8,128)(2,1)}, u32[]{:S(2)}, u32[]{:S(2)}) %collective-permute-start.7) | collective-permute-done | bytes 5308448 | tf_op jit(solution)/shard_map/ppermute | solution.py:249
  353.7 0.0 copy-start.2
  353.7 30.9 %adamw.5 = (f32[2,1152,1152]{2,1,0:T(8,128)}, f32[2,1152,1152]{2,1,0:T(8,128)}, bf16[2,4608,1152]{2,1,0:T(8,128)(2,1)}, bf16[2304,1152]{1,0:T(8,128)(2,1)}, bf16...) custom-call(s32[4]{0:T(128)} %iota_xor_fusion.where_ref.refs_4_, ...), custom_call_target="tpu_custom_call" | custom-call | flops 10000000000 | bytes 100000000 | tf_op jit(solution)/shard_map/adamw/pallas_call | solution.py:176
  384.6 1.5 collective-permute-start.13
  386.1 81.3 %collective-permute-done.1.refs_1_ = bf16[576,4608]{1,0:T(8,128)(2,1)} collective-permute-done((bf16[576,4608]{1,0:T(8,128)(2,1)}, bf16[576,4608]{1,0:T(8,128)(2,1)}, u32[]{:S(2)}, u32[]{:S(2)}) %collective-permute-start.1) | collective-permute-done | bytes 5308448 | tf_op jit(solution)/shard_map/ppermute | solution.py:249
  467.4 0.0 collective-permute-start.2
  467.5 1.5 collective-permute-start.11
  468.9 0.0 collective-permute-done.refs_0_
  468.9 0.6 collective-permute-start.9
  469.5 159.0 %collective-permute-done.11.refs_1_ = bf16[192,1152]{1,0:T(8,128)(2,1)S(1)} collective-permute-done((bf16[192,1152]{1,0:T(8,128)(2,1)}, bf16[192,1152]{1,0:T(8,128)(2,1)S(1)}, u32[]{:S(2)}, u32[]{:S(2)}) %collective-permute-start.11) | collective-permute-done | bytes 442400 | tf_op jit(solution)/shard_map/ppermute | solution.py:249
  628.5 0.0 collective-permute-start.4
  628.5 0.0 collective-permute-done.5.refs_1_
  628.5 0.5 collective-permute-start.6
  629.0 8.0 %collective-permute-done.9.refs_1_ = bf16[192,1152]{1,0:T(8,128)(2,1)} collective-permute-done((bf16[192,1152]{1,0:T(8,128)(2,1)}, bf16[192,1152]{1,0:T(8,128)(2,1)}, u32[]{:S(2)}, u32[]{:S(2)}) %collective-permute-start.9) | collective-permute-done | bytes 442400 | tf_op jit(solution)/shard_map/ppermute | solution.py:249
  637.0 0.0 collective-permute-start.8
  637.0 0.0 collective-permute-done.13.refs_1_
  637.0 1.7 collective-permute-start.15
  638.7 58.5 %collective-permute-done.15.refs_1_ = bf16[1152,1152]{1,0:T(8,128)(2,1)S(1)} collective-permute-done((bf16[1152,1152]{1,0:T(8,128)(2,1)}, bf16[1152,1152]{1,0:T(8,128)(2,1)S(1)}, u32[]{:S(2)}, u32[]{:S(2)}) %collective-permute-start.15) | collective-permute-done | bytes 2654240 | tf_op jit(solution)/shard_map/ppermute | solution.py:249
  697.2 0.0 collective-permute-start.16
  697.2 0.0 collective-permute-done.2.refs_2_
  697.2 0.5 collective-permute-start.14
  697.7 0.0 collective-permute-done.4.refs_0_
  697.7 0.0 collective-permute-start.12
  697.7 0.0 collective-permute-done.6.refs_2_
  697.7 0.5 collective-permute-start.10
  698.2 0.0 copy-done.2
  698.2 26.6 %put.6.refs_4_ = bf16[2,1152,4608]{2,1,0:T(8,128)(2,1)} custom-call(s32[4]{0:T(128)S(1)} %copy-done.2, bf16[576,4608]{1,0:T(8,128)(2,1)} %collective-permute-done.refs_0_, bf16[576,4608]{1,0:T(8,128)(2,1)} %collective-permute-done.1.refs_1_, bf16[576,4608]{1,0:T(8,128)(2,1)S(1)} %collective-permute-done.2.refs_2_, ...), custom_call_target="tpu_custom_call", output_to_operand_aliasing={{}: (4, {})} | custom-call | flops 1000000000 | bytes 10000000 | tf_op jit(solution)/shard_map/put/pallas_call | solution.py:232
  724.8 0.0 copy-start.1
  724.8 7.0 copy-done.1
  731.8 25.0 %put.7.refs_4_ = bf16[2,1152,4608]{2,1,0:T(8,128)(2,1)} custom-call(s32[4]{0:T(128)S(1)} %copy-done.2, bf16[576,4608]{1,0:T(8,128)(2,1)S(1)} %collective-permute-done.4.refs_0_, bf16[576,4608]{1,0:T(8,128)(2,1)} %collective-permute-done.5.refs_1_, bf16[576,4608]{1,0:T(8,128)(2,1)S(1)} %collective-permute-done.6.refs_2_, ...), custom_call_target="tpu_custom_call", output_to_operand_aliasing={{}: (4, {})} | custom-call | flops 1000000000 | bytes 10000000 | tf_op jit(solution)/shard_map/put/pallas_call | solution.py:232
  756.8 0.0 collective-permute-done.8.refs_0_
  756.8 0.0 collective-permute-done.16.refs_2_
  756.8 0.0 copy-start
  756.8 7.0 copy-done
  763.8 8.0 %put.8.refs_3_ = bf16[2,4608,1152]{2,1,0:T(8,128)(2,1)} custom-call(s32[4]{0:T(128)S(1)} %copy-done.2, bf16[2304,1152]{1,0:T(8,128)(2,1)S(1)} %collective-permute-done.8.refs_0_, bf16[1152,1152]{1,0:T(8,128)(2,1)S(1)} %collective-permute-done.15.refs_1_, bf16[1152,1152]{1,0:T(8,128)(2,1)S(1)} %collective-permute-done.16.refs_2_, ...), custom_call_target="tpu_custom_call", output_to_operand_aliasing={{}: (4, {})} | custom-call | flops 1000000000 | bytes 10000000 | tf_op jit(solution)/shard_map/put/pallas_call | solution.py:232
  771.8 0.0 collective-permute-done.14.refs_2_
  771.8 9.2 %put.9.refs_3_ = bf16[2,4608,1152]{2,1,0:T(8,128)(2,1)} custom-call(s32[4]{0:T(128)S(1)} %copy-done.2, bf16[2304,1152]{1,0:T(8,128)(2,1)S(1)} %collective-permute-done.8.refs_0_, bf16[768,1152]{1,0:T(8,128)(2,1)S(1)} %collective-permute-done.13.refs_1_, bf16[768,1152]{1,0:T(8,128)(2,1)} %collective-permute-done.14.refs_2_, ...), custom_call_target="tpu_custom_call", output_to_operand_aliasing={{}: (4, {})} | custom-call | flops 1000000000 | bytes 10000000 | tf_op jit(solution)/shard_map/put/pallas_call | solution.py:232
  781.0 0.0 collective-permute-done.12.refs_2_
  781.0 3.2 put.10.refs_3_
  784.2 0.0 collective-permute-done.10.refs_2_
  784.2 3.3 put.11
Async XLA Ops:
  122.3 117.7 %collective-permute-start.3 = (bf16[2,288,4608]{2,1,0:T(8,128)(2,1)}, bf16[2,288,4608]{2,1,0:T(8,128)(2,1)}, u32[]{:S(2)}, u32[]{:S(2)}) collective-permute-start(bf16[2,288,4608]{2,1,0:T(8,128)(2,1)} %get-tuple-element.36), channel_id=1, source_target_pairs={{0,2},{1,3},{2,0},{3,1},{4,6},{5,7},{6,4},{7,5}} | collective-permute-start | bytes 15925256 | tf_op jit(solution)/shard_map/ppermute | solution.py:249
  123.8 229.9 %collective-permute-start.7 = (bf16[2,1152,1152]{2,1,0:T(8,128)(2,1)}, bf16[2,1152,1152]{2,1,0:T(8,128)(2,1)}, u32[]{:S(2)}, u32[]{:S(2)}) collective-permute-start(bf16[2,1152,1152]{2,1,0:T(8,128)(2,1)} %get-tuple-element.40), channel_id=1, source_target_pairs={{0,2},{1,3},{2,0},{3,1},{4,6},{5,7},{6,4},{7,5}} | collective-permute-start | bytes 15925256 | tf_op jit(solution)/shard_map/ppermute | solution.py:249
  153.7 313.7 %collective-permute-start.1 = (bf16[576,4608]{1,0:T(8,128)(2,1)}, bf16[576,4608]{1,0:T(8,128)(2,1)}, u32[]{:S(2)}, u32[]{:S(2)}) collective-permute-start(bf16[576,4608]{1,0:T(8,128)(2,1)} %get-tuple-element.33), channel_id=1, source_target_pairs={{0,2},{1,3},{2,0},{3,1},{4,6},{5,7},{6,4},{7,5}} | collective-permute-start | bytes 15925256 | tf_op jit(solution)/shard_map/ppermute | solution.py:249
  155.2 313.7 %collective-permute-start = (bf16[576,4608]{1,0:T(8,128)(2,1)}, bf16[576,4608]{1,0:T(8,128)(2,1)}, u32[]{:S(2)}, u32[]{:S(2)}) collective-permute-start(bf16[576,4608]{1,0:T(8,128)(2,1)} %get-tuple-element.33), channel_id=1, source_target_pairs={{0,1},{1,0},{2,3},{3,2},{4,5},{5,4},{6,7},{7,6}} | collective-permute-start | bytes 15925256 | tf_op jit(solution)/shard_map/ppermute | solution.py:249
  268.8 359.7 %collective-permute-start.5 = (bf16[576,4608]{1,0:T(8,128)(2,1)}, bf16[576,4608]{1,0:T(8,128)(2,1)}, u32[]{:S(2)}, u32[]{:S(2)}) collective-permute-start(bf16[576,4608]{1,0:T(8,128)(2,1)} %get-tuple-element.37), channel_id=1, source_target_pairs={{0,2},{1,3},{2,0},{3,1},{4,6},{5,7},{6,4},{7,5}} | collective-permute-start | bytes 15925256 | tf_op jit(solution)/shard_map/ppermute | solution.py:249
  353.7 344.5 %copy-start.2 = (s32[4]{0:T(128)S(1)}, s32[4]{0:T(128)}, u32[]{:S(2)}) copy-start(s32[4]{0:T(128)} %iota_xor_fusion.where_ref.refs_4_) | copy-start | bytes 52
  384.6 252.3 %collective-permute-start.13 = (bf16[768,1152]{1,0:T(8,128)(2,1)}, bf16[768,1152]{1,0:T(8,128)(2,1)S(1)}, u32[]{:S(2)}, u32[]{:S(2)}) collective-permute-start(bf16[768,1152]{1,0:T(8,128)(2,1)} %get-tuple-element.44), channel_id=1, source_target_pairs={{0,2},{1,3},{2,0},{3,1},{4,6},{5,7},{6,4},{7,5}} | collective-permute-start | bytes 5308424 | tf_op jit(solution)/shard_map/ppermute | solution.py:249
  467.4 229.7 %collective-permute-start.2 = (bf16[576,4608]{1,0:T(8,128)(2,1)}, bf16[576,4608]{1,0:T(8,128)(2,1)S(1)}, u32[]{:S(2)}, u32[]{:S(2)}) collective-permute-start(bf16[576,4608]{1,0:T(8,128)(2,1)} %collective-permute-done.1.refs_1_), channel_id=1, source_target_pairs={{0,1},{1,0},{2,3},{3,2},{4,5},{5,4},{6,7},{7,6}} | collective-permute-start | bytes 15925256 | tf_op jit(solution)/shard_map/ppermute | solution.py:249
  467.5 161.0 %collective-permute-start.11 = (bf16[192,1152]{1,0:T(8,128)(2,1)}, bf16[192,1152]{1,0:T(8,128)(2,1)S(1)}, u32[]{:S(2)}, u32[]{:S(2)}) collective-permute-start(bf16[192,1152]{1,0:T(8,128)(2,1)} %get-tuple-element.43), channel_id=1, source_target_pairs={{0,2},{1,3},{2,0},{3,1},{4,6},{5,7},{6,4},{7,5}} | collective-permute-start | bytes 1327112 | tf_op jit(solution)/shard_map/ppermute | solution.py:249
  468.9 168.0 %collective-permute-start.9 = (bf16[192,1152]{1,0:T(8,128)(2,1)}, bf16[192,1152]{1,0:T(8,128)(2,1)}, u32[]{:S(2)}, u32[]{:S(2)}) collective-permute-start(bf16[192,1152]{1,0:T(8,128)(2,1)} %get-tuple-element.42), channel_id=1, source_target_pairs={{0,2},{1,3},{2,0},{3,1},{4,6},{5,7},{6,4},{7,5}} | collective-permute-start | bytes 1327112 | tf_op jit(solution)/shard_map/ppermute | solution.py:249
  628.5 69.2 %collective-permute-start.4 = (bf16[576,4608]{1,0:T(8,128)(2,1)}, bf16[576,4608]{1,0:T(8,128)(2,1)S(1)}, u32[]{:S(2)}, u32[]{:S(2)}) collective-permute-start(bf16[576,4608]{1,0:T(8,128)(2,1)} %get-tuple-element.37), channel_id=1, source_target_pairs={{0,1},{1,0},{2,3},{3,2},{4,5},{5,4},{6,7},{7,6}} | collective-permute-start | bytes 15925256 | tf_op jit(solution)/shard_map/ppermute | solution.py:249
  628.5 69.2 %collective-permute-start.6 = (bf16[576,4608]{1,0:T(8,128)(2,1)}, bf16[576,4608]{1,0:T(8,128)(2,1)S(1)}, u32[]{:S(2)}, u32[]{:S(2)}) collective-permute-start(bf16[576,4608]{1,0:T(8,128)(2,1)} %collective-permute-done.5.refs_1_), channel_id=1, source_target_pairs={{0,1},{1,0},{2,3},{3,2},{4,5},{5,4},{6,7},{7,6}} | collective-permute-start | bytes 15925256 | tf_op jit(solution)/shard_map/ppermute | solution.py:249
  637.0 119.8 %collective-permute-start.8 = (bf16[2304,1152]{1,0:T(8,128)(2,1)}, bf16[2304,1152]{1,0:T(8,128)(2,1)S(1)}, u32[]{:S(2)}, u32[]{:S(2)}) collective-permute-start(bf16[2304,1152]{1,0:T(8,128)(2,1)} %get-tuple-element.41), channel_id=1, source_target_pairs={{0,1},{1,0},{2,3},{3,2},{4,5},{5,4},{6,7},{7,6}} | collective-permute-start | bytes 15925256 | tf_op jit(solution)/shard_map/ppermute | solution.py:249
  637.0 60.2 %collective-permute-start.15 = (bf16[1152,1152]{1,0:T(8,128)(2,1)}, bf16[1152,1152]{1,0:T(8,128)(2,1)S(1)}, u32[]{:S(2)}, u32[]{:S(2)}) collective-permute-start(bf16[1152,1152]{1,0:T(8,128)(2,1)} %get-tuple-element.45), channel_id=1, source_target_pairs={{0,2},{1,3},{2,0},{3,1},{4,6},{5,7},{6,4},{7,5}} | collective-permute-start | bytes 7962632 | tf_op jit(solution)/shard_map/ppermute | solution.py:249
  697.2 59.6 %collective-permute-start.16 = (bf16[1152,1152]{1,0:T(8,128)(2,1)S(1)}, bf16[1152,1152]{1,0:T(8,128)(2,1)S(1)}, u32[]{:S(2)}, u32[]{:S(2)}) collective-permute-start(bf16[1152,1152]{1,0:T(8,128)(2,1)S(1)} %collective-permute-done.15.refs_1_), channel_id=1, source_target_pairs={{0,1},{1,0},{2,3},{3,2},{4,5},{5,4},{6,7},{7,6}} | collective-permute-start | bytes 7962632 | tf_op jit(solution)/shard_map/ppermute | solution.py:249
  697.2 74.7 %collective-permute-start.14 = (bf16[768,1152]{1,0:T(8,128)(2,1)S(1)}, bf16[768,1152]{1,0:T(8,128)(2,1)}, u32[]{:S(2)}, u32[]{:S(2)}) collective-permute-start(bf16[768,1152]{1,0:T(8,128)(2,1)S(1)} %collective-permute-done.13.refs_1_), channel_id=1, source_target_pairs={{0,1},{1,0},{2,3},{3,2},{4,5},{5,4},{6,7},{7,6}} | collective-permute-start | bytes 5308424 | tf_op jit(solution)/shard_map/ppermute | solution.py:249
  697.7 83.3 %collective-permute-start.12 = (bf16[192,1152]{1,0:T(8,128)(2,1)S(1)}, bf16[192,1152]{1,0:T(8,128)(2,1)}, u32[]{:S(2)}, u32[]{:S(2)}) collective-permute-start(bf16[192,1152]{1,0:T(8,128)(2,1)S(1)} %collective-permute-done.11.refs_1_), channel_id=1, source_target_pairs={{0,1},{1,0},{2,3},{3,2},{4,5},{5,4},{6,7},{7,6}} | collective-permute-start | bytes 1327112 | tf_op jit(solution)/shard_map/ppermute | solution.py:249
  697.7 86.5 %collective-permute-start.10 = (bf16[192,1152]{1,0:T(8,128)(2,1)}, bf16[192,1152]{1,0:T(8,128)(2,1)}, u32[]{:S(2)}, u32[]{:S(2)}) collective-permute-start(bf16[192,1152]{1,0:T(8,128)(2,1)} %collective-permute-done.9.refs_1_), channel_id=1, source_target_pairs={{0,1},{1,0},{2,3},{3,2},{4,5},{5,4},{6,7},{7,6}} | collective-permute-start | bytes 1327112 | tf_op jit(solution)/shard_map/ppermute | solution.py:249
  724.8 7.0 copy-start.1
  756.8 7.0 copy-start

commit v2 on v1

--- a/solution.py
+++ b/solution.py
@@ -9,7 +9,10 @@
 MESH = pl.DeviceIdType.MESH
 BF16, F32 = jnp.bfloat16, jnp.float32
 ANY = pl.BlockSpec(memory_space=pl.ANY)
-PER_LAYER = 6
+HBM = pl.BlockSpec(memory_space=pltpu.HBM)
+SUM_PIECES = (9, 6, 6)
+STEP_PIECES = (6, 6, 12)
+LATE = 12
 
 
 PARTNER = [(i, i ^ 1) for i in range(4)]
@@ -22,7 +25,8 @@
     theirs = refs[4:7]
     sums = (None, *refs[7:9])
     mine, landed = refs[9:12], refs[12:15]
-    in_send, in_recv, load, out_send, out_recv, store, own_send, own_recv = refs[15:]
+    in_send, in_recv, load = refs[15:18], refs[18:21], refs[21:24]
+    out_send, out_recv, store, own_send, own_recv = refs[24:]
 
     rep, me = lax.axis_index("rep"), lax.axis_index("dp")
     chip, core = me // 2, me % 2
@@ -30,26 +34,22 @@
     across = (1 - chip) * 2 + core
     diagonal = (1 - chip) * 2 + (1 - core)
 
-    barrier = pltpu.get_barrier_semaphore()
-    for other in (partner, across):
-        pl.semaphore_signal(barrier, inc=1, device_id=(rep, other), device_id_type=MESH)
-    pl.semaphore_wait(barrier, 2)
-
     def piece(w, owner, t):
         rows = mine[w].shape[1]
-        return g[w].at[0, t // PER_LAYER, pl.ds((owner * PER_LAYER + t % PER_LAYER) * rows, rows)]
+        return g[w].at[0, t // SUM_PIECES[w], pl.ds((owner * SUM_PIECES[w] + t % SUM_PIECES[w]) * rows, rows)]
 
     def place(ref, w, t):
         rows = mine[w].shape[1]
-        return ref.at[t // PER_LAYER, pl.ds((t % PER_LAYER) * rows, rows)]
+        return ref.at[t // SUM_PIECES[w], pl.ds((t % SUM_PIECES[w]) * rows, rows)]
 
     def to_partner(w, t):
+        sems = in_send[w].at[t], in_recv[w].at[t]
         return pltpu.make_async_remote_copy(
-            piece(w, diagonal, t), landed[w].at[t], in_send.at[w, t], in_recv.at[w, t], device_id=(rep, partner), device_id_type=MESH
+            piece(w, diagonal, t), landed[w].at[t], *sems, device_id=(rep, partner), device_id_type=MESH
         )
 
     def to_mine(w, t):
-        return pltpu.make_async_copy(piece(w, across, t), mine[w].at[t], load.at[w, t])
+        return pltpu.make_async_copy(piece(w, across, t), mine[w].at[t], load[w].at[t])
 
     def send_across(t):
         return pltpu.make_async_remote_copy(
@@ -70,18 +70,36 @@
         to_mine(w, t).wait()
         mine[w][t] = (mine[w][t].astype(F32) + landed[w][t].astype(F32)).astype(BF16)
 
-    pieces = 2 * PER_LAYER
-
-    @pl.loop(0, pieces)
-    def _(t):
-        to_partner(0, t).start()
-        to_mine(0, t).start()
-
-    @pl.loop(0, pieces)
+    def each(w, body):
+        pl.loop(0, 2 * SUM_PIECES[w])(body)
+
+    barrier = pltpu.get_barrier_semaphore()
+    for other in (partner, across):
+        pl.semaphore_signal(barrier, inc=1, device_id=(rep, other), device_id_type=MESH)
+    each(0, lambda t: to_mine(0, t).start())
+    pl.semaphore_wait(barrier, 2)
+    each(0, lambda t: to_partner(0, t).start())
+
+    @pl.loop(0, 2 * SUM_PIECES[0])
     def _(t):
         add(0, t)
-        send_across(t).start()
-        for w in (1, 2):
+
+        @pl.when(core == 1)
+        def _():
+            send_across(t).start()
+
+        @pl.when((core == 0) & (t >= LATE))
+        def _():
+            send_across(t - LATE).start()
+
+    @pl.when(core == 0)
+    def _():
+        pl.loop(2 * SUM_PIECES[0] - LATE, 2 * SUM_PIECES[0])(lambda t: send_across(t).start())
+
+    for w in (1, 2):
+
+        @pl.loop(0, 2 * SUM_PIECES[w])
+        def _(t, w=w):
             to_partner(w, t).start()
             to_mine(w, t).start()
 
@@ -90,31 +108,25 @@
 
     for w in (1, 2):
 
-        @pl.loop(0, pieces)
+        @pl.loop(0, 2 * SUM_PIECES[w])
         def _(t, w=w):
             add(w, t)
             keep(w, t).start()
 
-    @pl.loop(0, pieces)
-    def _(t):
-        for w in range(3):
-            to_partner(w, t).wait_send()
-        for w in (1, 2):
-            keep(w, t).wait()
-
+    for w in range(3):
+        each(w, lambda t, w=w: to_partner(w, t).wait_send())
+    for w in (1, 2):
+        each(w, lambda t, w=w: keep(w, t).wait())
     for w in range(3):
         own_terms(w).wait()
-
-    @pl.loop(0, pieces)
-    def _(t):
-        send_across(t).wait()
+    each(0, lambda t: send_across(t).wait())
 
 
 def exchange(terms, blocks):
     shapes = [(2, *b) for b in blocks]
-    vmem = [pltpu.VMEM((2 * PER_LAYER, b[0] // PER_LAYER, b[1]), BF16) for b in blocks]
-    pieces = 2 * PER_LAYER
+    vmem = [pltpu.VMEM((2 * n, b[0] // n, b[1]), BF16) for n, b in zip(SUM_PIECES, blocks, strict=True)]
     dma = pltpu.SemaphoreType.DMA
+    sems = [dma((2 * n,)) for n in SUM_PIECES]
     return pl.pallas_call(
         pair_sums,
         out_shape=[jax.ShapeDtypeStruct(s, BF16) for s in (shapes[0], *shapes, *shapes[1:])],
@@ -123,12 +135,12 @@
         scratch_shapes=[
             *vmem,
             *vmem,
-            dma((3, pieces)),
-            dma((3, pieces)),
-            dma((3, pieces)),
-            dma((pieces,)),
-            dma((pieces,)),
-            dma((2, pieces)),
+            *sems,
+            *sems,
+            *sems,
+            sems[0],
+            sems[0],
+            dma((2, 2 * max(SUM_PIECES[1:]))),
             dma((3,)),
             dma((3,)),
         ],
@@ -138,10 +150,10 @@
     )(*terms)
 
 
-def adamw(splits, where, g, theirs, arrived, m, v, w):
+def adamw(per, splits, where, g, theirs, arrived, m, v, w):
     layers, block, columns = m.shape
-    rows = block // PER_LAYER
-    steps = layers * PER_LAYER
+    rows = block // per
+    steps = layers * per
     firsts = [first // rows for first, _ in splits]
     counts = [size // rows for _, size in splits]
 
@@ -164,10 +176,10 @@
                 part[...] = new_w
 
     def own(i, where):
-        return (i // PER_LAYER, i % PER_LAYER, 0)
+        return (i // per, i % per, 0)
 
     def inside(i, where):
-        return (i // PER_LAYER, where[0] * PER_LAYER + i % PER_LAYER, 0)
+        return (i // per, where[0] * per + i % per, 0)
 
     def part_map(first, count):
         return lambda i, where: (jnp.clip(i - first, 0, count - 1), 0)
@@ -204,9 +216,9 @@
     )(where, g, theirs, arrived, m, v, w)
 
 
-def put(where, whole, after, block, first, arrived):
+def put(per, where, whole, after, block, first, arrived):
     columns = whole.shape[2]
-    rows = block // PER_LAYER
+    rows = block // per
     count = min(a.shape[0] for _, _, a in arrived) // rows
     n = len(arrived)
 
@@ -227,14 +239,14 @@
         owner = where[arrived[0][0]]
         for k in range(1, n):
             owner = jnp.where(j == k, where[arrived[k][0]], owner)
-        return (t // PER_LAYER, owner * PER_LAYER + t % PER_LAYER, 0)
+        return (t // per, owner * per + t % per, 0)
 
     return pl.pallas_call(
         body,
         grid_spec=pltpu.PrefetchScalarGridSpec(
             num_scalar_prefetch=1,
             grid=(count, n),
-            in_specs=[*(pl.BlockSpec((rows, columns), in_map(skip)) for _, skip, _ in arrived), ANY, ANY],
+            in_specs=[*(pl.BlockSpec((rows, columns), in_map(skip)) for _, skip, _ in arrived), HBM, HBM],
             out_specs=pl.BlockSpec((1, rows, columns), out_map),
         ),
         out_shape=jax.ShapeDtypeStruct(whole.shape, BF16),
@@ -245,8 +257,42 @@
     )(where, *(a for _, _, a in arrived), whole, after)
 
 
+def put_now(whole, block, first, arrived):
+    layer, row = first // block, first % block
+    size = arrived[0][1].shape[0]
+    n = len(arrived)
+
+    def body(*refs):
+        out, sems = refs[-2:]
+        me = lax.axis_index("dp")
+        chip, core = me // 2, me % 2
+        copies = []
+        for k, (which, _) in enumerate(arrived):
+            owner = (1 - chip if which // 2 else chip) * 2 + (1 - core if which % 2 else core)
+            copies.append(pltpu.make_async_copy(refs[k], out.at[layer, pl.ds(owner * block + row, size)], sems.at[k]))
+        for copy in copies:
+            copy.start()
+        for copy in copies:
+            copy.wait()
+
+    return pl.pallas_call(
+        body,
+        in_specs=[*(pl.BlockSpec(memory_space=pltpu.VMEM) for _ in range(n)), HBM],
+        out_specs=HBM,
+        out_shape=jax.ShapeDtypeStruct(whole.shape, BF16),
+        scratch_shapes=[pltpu.SemaphoreType.DMA((n,))],
+        input_output_aliases={n: 0},
+        compiler_params=pltpu.CompilerParams(vmem_limit_bytes=16 << 20),
+        cost_estimate=pl.CostEstimate(flops=10**9, bytes_accessed=10**7, transcendentals=0),
+        name="put_now",
+    )(*(a for _, a in arrived), whole)
+
+
 def send(array, pairs):
     return lax.ppermute(array, "dp", pairs)
+
+
+LAST = (12, 6, 3, 2, 1)
 
 
 def solution(mesh):
@@ -261,19 +307,26 @@
         after = where
         for k in range(3):
             block = blocks[k][0]
-            rows = block // PER_LAYER
+            per = STEP_PIECES[k]
+            rows = block // per
             splits = [(0, 2 * block)]
             if k == 2:
-                sizes = (block, 4 * rows, rows, rows)
-                splits += [(sum(sizes[:i]), sizes[i]) for i in range(4)]
-            m, v, w, block_w, *parts = adamw(splits, where, terms[k], theirs[k], arrived[k], ms[k], vs[k], weights[k])
+                splits += [(sum(LAST[:i]) * rows, LAST[i] * rows) for i in range(len(LAST))]
+            m, v, w, block_w, *parts = adamw(per, splits, where, terms[k], theirs[k], arrived[k], ms[k], vs[k], weights[k])
             parts = parts or [block_w]
             over = [send(a, ACROSS) for a in parts]
             beside = send(block_w, PARTNER)
             passed = [send(a, PARTNER) for a in over]
+            if k == 2:
+                w = put(per, where, w, new_w[0], block, 0, [(1, 0, beside)])
             first = 0
-            for a, b in zip(over, passed, strict=True):
-                w = put(where, w, after, block, first, [(1, first, beside), (2, 0, a), (3, 0, b)])
+            for i, (a, b) in enumerate(zip(over, passed, strict=True)):
+                if k < 2:
+                    w = put(per, where, w, after, block, first, [(1, first, beside), (2, 0, a), (3, 0, b)])
+                elif LAST[i] > 3:
+                    w = put(per, where, w, after, block, first, [(2, 0, a), (3, 0, b)])
+                else:
+                    w = put_now(w, block, first, [(2, a), (3, b)])
                 first += a.shape[0]
             after = w
             new_w.append(w)

time: 789 us -> 787 us (level)
  waiting for transfers between devices: 475 us -> 462 us
  Pallas kernels: 286 us -> 294 us
    ppermute x17 -> x19, waiting for transfers between devices: 475 us -> 462 us  [send(): return lax.ppermute(array, 'dp', pairs)]
    pallas_call x6 -> x5, Pallas kernels: 75.2 us -> 74.8 us  [put(): pl.pallas_call(body, grid_spec=pltpu.PrefetchScalarGridSpec(num_scalar_pr...]
  transfers between devices with their start and end apart: 17 -> 19, of which waited for: 6 -> 7; matrix products, arithmetic and copies ran while one was open for 0% -> 0% of each run, Pallas kernels for 20% -> 22%
where the time goes in v2:
time: 787 us; the launch traced here: 786 us
  waiting for transfers between devices  462 us (59%)
  Pallas kernels  294 us (37%)
  starting transfers between devices  14.3 us (2%)
  local copies, waits for them, and re-layouts  14.1 us (2%)
    ppermute x19, waiting for transfers between devices, send(): return lax.ppermute(array, 'dp', pairs)  462 us
    pallas_call x1, Pallas kernels, exchange(): pl.pallas_call(pair_sums, out_shape=[jax.ShapeDtypeStruct(s, BF16) for s...  122 us
    pallas_call x3, Pallas kernels, adamw(): pl.pallas_call(body, grid_spec=pltpu.PrefetchScalarGridSpec(num_scalar_pr...  94.2 us
    pallas_call x5, Pallas kernels, put(): pl.pallas_call(body, grid_spec=pltpu.PrefetchScalarGridSpec(num_scalar_pr...  74.8 us
  transfers between devices with their start and end apart: 19, of which 7 were waited for; matrix products, arithmetic and copies ran while one was open for 0% of the time, Pallas kernels for 22%

profile of v2, /device:TPU:0, one launch (start us, length us, event | category | flops | bytes accessed | tf_op | source)
XLA Modules:
  0.0 785.7 jit_solution(15057243530996099623)
XLA Ops:
  0.6 122.0 %pair_sums.1 = (bf16[2,288,4608]{2,1,0:T(8,128)(2,1)}, bf16[2,288,4608]{2,1,0:T(8,128)(2,1)}, bf16[2,288,4608]{2,1,0:T(8,128)(2,1)}, bf16[2,1152,1152]{2,1,0:T(8...) custom-call(bf16[1,2,1152,4608]{3,2,1,0:T(8,128)(2,1)} %g_ref.3, ...), custom_call_target="tpu_custom_call" | custom-call | flops 100000000 | bytes 100000000 | tf_op jit(solution)/shard_map/pair_sums/pallas_call | solution.py:130
  122.6 1.8 collective-permute-start.3
  124.4 0.3 collective-permute-start.7
  124.7 0.5 iota_xor_fusion.where_ref.refs_4_
  125.2 28.8 %adamw.3 = (f32[2,288,4608]{2,1,0:T(8,128)}, f32[2,288,4608]{2,1,0:T(8,128)}, bf16[2,1152,4608]{2,1,0:T(8,128)(2,1)}, bf16[576,4608]{1,0:T(8,128)(2,1)}) custom-call(s32[4]{0:T(128)} %iota_xor_fusion.where_ref.refs_4_, bf16[1,2,1152,4608]{3,2,1,0:T(8,128)(2,1)} %g_ref.3, bf16[2,288,4608]{2,1,0:T(8,128)(2,1)} %get-tuple-element.32.theirs_ref, ...), custom_call_target="tpu_custom_call" | custom-call | flops 10000000000 | bytes 100000000 | tf_op jit(solution)/shard_map/adamw/pallas_call | solution.py:188
  154.0 1.7 collective-permute-start.1
  155.8 0.0 collective-permute-start
  155.8 84.5 %collective-permute-done.3.arrived_ref = bf16[2,288,4608]{2,1,0:T(8,128)(2,1)} collective-permute-done((bf16[2,288,4608]{2,1,0:T(8,128)(2,1)}, bf16[2,288,4608]{2,1,0:T(8,128)(2,1)}, u32[]{:S(2)}, u32[]{:S(2)}) %collective-permute-start.3) | collective-permute-done | bytes 5308448 | tf_op jit(solution)/shard_map/ppermute | solution.py:292
  240.3 28.9 %adamw.4 = (f32[2,288,4608]{2,1,0:T(8,128)}, f32[2,288,4608]{2,1,0:T(8,128)}, bf16[2,1152,4608]{2,1,0:T(8,128)(2,1)}, bf16[576,4608]{1,0:T(8,128)(2,1)}) custom-call(s32[4]{0:T(128)} %iota_xor_fusion.where_ref.refs_4_, bf16[1,2,1152,4608]{3,2,1,0:T(8,128)(2,1)} %g_ref.4, bf16[2,288,4608]{2,1,0:T(8,128)(2,1)} %get-tuple-element.36.theirs_ref, ...), custom_call_target="tpu_custom_call" | custom-call | flops 10000000000 | bytes 100000000 | tf_op jit(solution)/shard_map/adamw/pallas_call | solution.py:188
  269.1 1.7 collective-permute-start.5
  270.8 83.2 %collective-permute-done.7.arrived_ref = bf16[2,1152,1152]{2,1,0:T(8,128)(2,1)} collective-permute-done((bf16[2,1152,1152]{2,1,0:T(8,128)(2,1)}, bf16[2,1152,1152]{2,1,0:T(8,128)(2,1)}, u32[]{:S(2)}, u32[]{:S(2)}) %collective-permute-start.7) | collective-permute-done | bytes 5308448 | tf_op jit(solution)/shard_map/ppermute | solution.py:292
  354.0 0.0 copy-start.2
  354.0 36.5 %adamw.5 = (f32[2,1152,1152]{2,1,0:T(8,128)}, f32[2,1152,1152]{2,1,0:T(8,128)}, bf16[2,4608,1152]{2,1,0:T(8,128)(2,1)}, bf16[2304,1152]{1,0:T(8,128)(2,1)}, bf16...) custom-call(s32[4]{0:T(128)} %iota_xor_fusion.where_ref.refs_4_, ...), custom_call_target="tpu_custom_call" | custom-call | flops 10000000000 | bytes 100000000 | tf_op jit(solution)/shard_map/adamw/pallas_call | solution.py:188
  390.6 1.8 collective-permute-start.14
  392.3 0.0 collective-permute-start.4
  392.3 75.5 %collective-permute-done.1.refs_1_ = bf16[576,4608]{1,0:T(8,128)(2,1)} collective-permute-done((bf16[576,4608]{1,0:T(8,128)(2,1)}, bf16[576,4608]{1,0:T(8,128)(2,1)}, u32[]{:S(2)}, u32[]{:S(2)}) %collective-permute-start.1) | collective-permute-done | bytes 5308448 | tf_op jit(solution)/shard_map/ppermute | solution.py:292
  467.8 1.7 collective-permute-start.8
  469.5 0.0 collective-permute-done.refs_0_
  469.5 0.3 collective-permute-start.10
  469.8 144.8 %collective-permute-done.8.refs_0_ = bf16[96,1152]{1,0:T(8,128)(2,1)S(1)} collective-permute-done((bf16[96,1152]{1,0:T(8,128)(2,1)}, bf16[96,1152]{1,0:T(8,128)(2,1)S(1)}, u32[]{:S(2)}, u32[]{:S(2)}) %collective-permute-start.8) | collective-permute-done | bytes 221216 | tf_op jit(solution)/shard_map/ppermute | solution.py:292
  614.6 1.7 collective-permute-start.12
  616.3 7.7 collective-permute-done.10.refs_0_
  624.1 0.0 collective-permute-start.2
  624.1 8.6 %collective-permute-done.12.refs_0_ = bf16[288,1152]{1,0:T(8,128)(2,1)S(1)} collective-permute-done((bf16[288,1152]{1,0:T(8,128)(2,1)}, bf16[288,1152]{1,0:T(8,128)(2,1)S(1)}, u32[]{:S(2)}, u32[]{:S(2)}) %collective-permute-start.12) | collective-permute-done | bytes 663584 | tf_op jit(solution)/shard_map/ppermute | solution.py:292
  632.7 0.0 collective-permute-start.18
  632.7 0.0 collective-permute-done.5.refs_1_
  632.7 0.5 collective-permute-start.6
  633.2 0.0 collective-permute-done.14.refs_0_
  633.2 1.7 collective-permute-start.16
  634.9 58.0 %collective-permute-done.16.refs_0_ = bf16[1152,1152]{1,0:T(8,128)(2,1)S(1)} collective-permute-done((bf16[1152,1152]{1,0:T(8,128)(2,1)}, bf16[1152,1152]{1,0:T(8,128)(2,1)S(1)}, u32[]{:S(2)}, u32[]{:S(2)}) %collective-permute-start.16) | collective-permute-done | bytes 2654240 | tf_op jit(solution)/shard_map/ppermute | solution.py:292
  692.9 0.0 collective-permute-start.17
  692.9 0.0 collective-permute-done.4.refs_0_
  692.9 0.5 collective-permute-start.15
  693.4 0.0 collective-permute-done.2.refs_2_
  693.4 0.0 collective-permute-start.13
  693.4 0.0 copy-done.2
  693.4 26.6 %put.5.refs_4_.refs_2_ = bf16[2,1152,4608]{2,1,0:T(8,128)(2,1)} custom-call(s32[4]{0:T(128)S(1)} %copy-done.2, bf16[576,4608]{1,0:T(8,128)(2,1)} %collective-permute-done.refs_0_, bf16[576,4608]{1,0:T(8,128)(2,1)} %collective-permute-done.1.refs_1_, bf16[576,4608]{1,0:T(8,128)(2,1)S(1)} %collective-permute-done.2.refs_2_, ...), custom_call_target="tpu_custom_call", output_to_operand_aliasing={{}: (4, {})} | custom-call | flops 1000000000 | bytes 10000000 | tf_op jit(solution)/shard_map/put/pallas_call | solution.py:244
  720.0 0.0 collective-permute-done.18.refs_0_
  720.0 0.5 collective-permute-start.11
  720.5 0.0 copy-start.1
  720.5 7.0 copy-done.1
  727.5 9.1 %put.7.refs_2_ = bf16[2,4608,1152]{2,1,0:T(8,128)(2,1)} custom-call(s32[4]{0:T(128)S(1)} %copy-done.2, bf16[2304,1152]{1,0:T(8,128)(2,1)S(1)} %collective-permute-done.18.refs_0_, bf16[2,4608,1152]{2,1,0:T(8,128)(2,1)} %get-tuple-element.48.refs_1_, bf16[2,1152,4608]{2,1,0:T(8,128)(2,1)S(1)} %copy-done.1), custom_call_target="tpu_custom_call", output_to_operand_aliasing={{}: (2, {})} | custom-call | flops 1000000000 | bytes 10000000 | tf_op jit(solution)/shard_map/put/pallas_call | solution.py:244
  736.6 0.0 collective-permute-done.6.refs_2_
  736.6 0.0 collective-permute-start.9
  736.6 25.0 %put.6.refs_3_ = bf16[2,1152,4608]{2,1,0:T(8,128)(2,1)} custom-call(s32[4]{0:T(128)S(1)} %copy-done.2, bf16[576,4608]{1,0:T(8,128)(2,1)S(1)} %collective-permute-done.4.refs_0_, bf16[576,4608]{1,0:T(8,128)(2,1)} %collective-permute-done.5.refs_1_, bf16[576,4608]{1,0:T(8,128)(2,1)S(1)} %collective-permute-done.6.refs_2_, ...), custom_call_target="tpu_custom_call", output_to_operand_aliasing={{}: (4, {})} | custom-call | flops 1000000000 | bytes 10000000 | tf_op jit(solution)/shard_map/put/pallas_call | solution.py:244
  761.6 0.0 collective-permute-done.17.refs_1_
  761.6 0.0 copy-start
  761.6 7.0 copy-done
  768.6 9.2 %put.8.refs_2_ = bf16[2,4608,1152]{2,1,0:T(8,128)(2,1)} custom-call(s32[4]{0:T(128)S(1)} %copy-done.2, bf16[1152,1152]{1,0:T(8,128)(2,1)S(1)} %collective-permute-done.16.refs_0_, bf16[1152,1152]{1,0:T(8,128)(2,1)S(1)} %collective-permute-done.17.refs_1_, bf16[2,4608,1152]{2,1,0:T(8,128)(2,1)} %put.7.refs_2_, ...), custom_call_target="tpu_custom_call", output_to_operand_aliasing={{}: (3, {})} | custom-call | flops 1000000000 | bytes 10000000 | tf_op jit(solution)/shard_map/put/pallas_call | solution.py:244
  777.8 0.0 collective-permute-done.15.refs_1_
  777.8 5.0 put.9.refs_2_
  782.8 0.0 collective-permute-done.13.refs_1_
  782.8 1.1 put_now.3.refs_2_
  783.9 0.0 collective-permute-done.11.refs_1_
  783.9 0.9 put_now.4.refs_2_
  784.9 0.0 collective-permute-done.9.refs_1_
  784.9 0.8 put_now.5
Async XLA Ops:
  122.6 117.7 %collective-permute-start.3 = (bf16[2,288,4608]{2,1,0:T(8,128)(2,1)}, bf16[2,288,4608]{2,1,0:T(8,128)(2,1)}, u32[]{:S(2)}, u32[]{:S(2)}) collective-permute-start(bf16[2,288,4608]{2,1,0:T(8,128)(2,1)} %get-tuple-element.37), channel_id=1, source_target_pairs={{0,2},{1,3},{2,0},{3,1},{4,6},{5,7},{6,4},{7,5}} | collective-permute-start | bytes 15925256 | tf_op jit(solution)/shard_map/ppermute | solution.py:292
  124.4 229.7 %collective-permute-start.7 = (bf16[2,1152,1152]{2,1,0:T(8,128)(2,1)}, bf16[2,1152,1152]{2,1,0:T(8,128)(2,1)}, u32[]{:S(2)}, u32[]{:S(2)}) collective-permute-start(bf16[2,1152,1152]{2,1,0:T(8,128)(2,1)} %get-tuple-element.41), channel_id=1, source_target_pairs={{0,2},{1,3},{2,0},{3,1},{4,6},{5,7},{6,4},{7,5}} | collective-permute-start | bytes 15925256 | tf_op jit(solution)/shard_map/ppermute | solution.py:292
  154.0 313.7 %collective-permute-start.1 = (bf16[576,4608]{1,0:T(8,128)(2,1)}, bf16[576,4608]{1,0:T(8,128)(2,1)}, u32[]{:S(2)}, u32[]{:S(2)}) collective-permute-start(bf16[576,4608]{1,0:T(8,128)(2,1)} %get-tuple-element.34), channel_id=1, source_target_pairs={{0,2},{1,3},{2,0},{3,1},{4,6},{5,7},{6,4},{7,5}} | collective-permute-start | bytes 15925256 | tf_op jit(solution)/shard_map/ppermute | solution.py:292
  155.8 313.8 %collective-permute-start = (bf16[576,4608]{1,0:T(8,128)(2,1)}, bf16[576,4608]{1,0:T(8,128)(2,1)}, u32[]{:S(2)}, u32[]{:S(2)}) collective-permute-start(bf16[576,4608]{1,0:T(8,128)(2,1)} %get-tuple-element.34), channel_id=1, source_target_pairs={{0,1},{1,0},{2,3},{3,2},{4,5},{5,4},{6,7},{7,6}} | collective-permute-start | bytes 15925256 | tf_op jit(solution)/shard_map/ppermute | solution.py:292
  269.1 363.5 %collective-permute-start.5 = (bf16[576,4608]{1,0:T(8,128)(2,1)}, bf16[576,4608]{1,0:T(8,128)(2,1)}, u32[]{:S(2)}, u32[]{:S(2)}) collective-permute-start(bf16[576,4608]{1,0:T(8,128)(2,1)} %get-tuple-element.38), channel_id=1, source_target_pairs={{0,2},{1,3},{2,0},{3,1},{4,6},{5,7},{6,4},{7,5}} | collective-permute-start | bytes 15925256 | tf_op jit(solution)/shard_map/ppermute | solution.py:292
  354.0 339.4 %copy-start.2 = (s32[4]{0:T(128)S(1)}, s32[4]{0:T(128)}, u32[]{:S(2)}) copy-start(s32[4]{0:T(128)} %iota_xor_fusion.where_ref.refs_4_) | copy-start | bytes 52
  390.6 242.6 %collective-permute-start.14 = (bf16[576,1152]{1,0:T(8,128)(2,1)}, bf16[576,1152]{1,0:T(8,128)(2,1)S(1)}, u32[]{:S(2)}, u32[]{:S(2)}) collective-permute-start(bf16[576,1152]{1,0:T(8,128)(2,1)} %get-tuple-element.45), channel_id=1, source_target_pairs={{0,2},{1,3},{2,0},{3,1},{4,6},{5,7},{6,4},{7,5}} | collective-permute-start | bytes 3981320 | tf_op jit(solution)/shard_map/ppermute | solution.py:292
  392.3 300.6 %collective-permute-start.4 = (bf16[576,4608]{1,0:T(8,128)(2,1)}, bf16[576,4608]{1,0:T(8,128)(2,1)S(1)}, u32[]{:S(2)}, u32[]{:S(2)}) collective-permute-start(bf16[576,4608]{1,0:T(8,128)(2,1)} %get-tuple-element.38), channel_id=1, source_target_pairs={{0,1},{1,0},{2,3},{3,2},{4,5},{5,4},{6,7},{7,6}} | collective-permute-start | bytes 15925256 | tf_op jit(solution)/shard_map/ppermute | solution.py:292
  467.8 146.8 %collective-permute-start.8 = (bf16[96,1152]{1,0:T(8,128)(2,1)}, bf16[96,1152]{1,0:T(8,128)(2,1)S(1)}, u32[]{:S(2)}, u32[]{:S(2)}) collective-permute-start(bf16[96,1152]{1,0:T(8,128)(2,1)} %get-tuple-element.42), channel_id=1, source_target_pairs={{0,2},{1,3},{2,0},{3,1},{4,6},{5,7},{6,4},{7,5}} | collective-permute-start | bytes 663560 | tf_op jit(solution)/shard_map/ppermute | solution.py:292
  469.5 154.6 %collective-permute-start.10 = (bf16[192,1152]{1,0:T(8,128)(2,1)}, bf16[192,1152]{1,0:T(8,128)(2,1)S(1)}, u32[]{:S(2)}, u32[]{:S(2)}) collective-permute-start(bf16[192,1152]{1,0:T(8,128)(2,1)} %get-tuple-element.43), channel_id=1, source_target_pairs={{0,2},{1,3},{2,0},{3,1},{4,6},{5,7},{6,4},{7,5}} | collective-permute-start | bytes 1327112 | tf_op jit(solution)/shard_map/ppermute | solution.py:292
  614.6 18.0 %collective-permute-start.12 = (bf16[288,1152]{1,0:T(8,128)(2,1)}, bf16[288,1152]{1,0:T(8,128)(2,1)S(1)}, u32[]{:S(2)}, u32[]{:S(2)}) collective-permute-start(bf16[288,1152]{1,0:T(8,128)(2,1)} %get-tuple-element.44), channel_id=1, source_target_pairs={{0,2},{1,3},{2,0},{3,1},{4,6},{5,7},{6,4},{7,5}} | collective-permute-start | bytes 1990664 | tf_op jit(solution)/shard_map/ppermute | solution.py:292
  624.1 69.3 %collective-permute-start.2 = (bf16[576,4608]{1,0:T(8,128)(2,1)}, bf16[576,4608]{1,0:T(8,128)(2,1)S(1)}, u32[]{:S(2)}, u32[]{:S(2)}) collective-permute-start(bf16[576,4608]{1,0:T(8,128)(2,1)} %collective-permute-done.1.refs_1_), channel_id=1, source_target_pairs={{0,1},{1,0},{2,3},{3,2},{4,5},{5,4},{6,7},{7,6}} | collective-permute-start | bytes 15925256 | tf_op jit(solution)/shard_map/ppermute | solution.py:292
  632.7 87.3 %collective-permute-start.18 = (bf16[2304,1152]{1,0:T(8,128)(2,1)}, bf16[2304,1152]{1,0:T(8,128)(2,1)S(1)}, u32[]{:S(2)}, u32[]{:S(2)}) collective-permute-start(bf16[2304,1152]{1,0:T(8,128)(2,1)} %get-tuple-element.47), channel_id=1, source_target_pairs={{0,1},{1,0},{2,3},{3,2},{4,5},{5,4},{6,7},{7,6}} | collective-permute-start | bytes 15925256 | tf_op jit(solution)/shard_map/ppermute | solution.py:292
  632.7 103.9 %collective-permute-start.6 = (bf16[576,4608]{1,0:T(8,128)(2,1)}, bf16[576,4608]{1,0:T(8,128)(2,1)S(1)}, u32[]{:S(2)}, u32[]{:S(2)}) collective-permute-start(bf16[576,4608]{1,0:T(8,128)(2,1)} %collective-permute-done.5.refs_1_), channel_id=1, source_target_pairs={{0,1},{1,0},{2,3},{3,2},{4,5},{5,4},{6,7},{7,6}} | collective-permute-start | bytes 15925256 | tf_op jit(solution)/shard_map/ppermute | solution.py:292
  633.2 59.7 %collective-permute-start.16 = (bf16[1152,1152]{1,0:T(8,128)(2,1)}, bf16[1152,1152]{1,0:T(8,128)(2,1)S(1)}, u32[]{:S(2)}, u32[]{:S(2)}) collective-permute-start(bf16[1152,1152]{1,0:T(8,128)(2,1)} %get-tuple-element.46), channel_id=1, source_target_pairs={{0,2},{1,3},{2,0},{3,1},{4,6},{5,7},{6,4},{7,5}} | collective-permute-start | bytes 7962632 | tf_op jit(solution)/shard_map/ppermute | solution.py:292
  692.9 68.7 %collective-permute-start.17 = (bf16[1152,1152]{1,0:T(8,128)(2,1)S(1)}, bf16[1152,1152]{1,0:T(8,128)(2,1)S(1)}, u32[]{:S(2)}, u32[]{:S(2)}) collective-permute-start(bf16[1152,1152]{1,0:T(8,128)(2,1)S(1)} %collective-permute-done.16.refs_0_), channel_id=1, source_target_pairs={{0,1},{1,0},{2,3},{3,2},{4,5},{5,4},{6,7},{7,6}} | collective-permute-start | bytes 7962632 | tf_op jit(solution)/shard_map/ppermute | solution.py:292
  692.9 85.0 %collective-permute-start.15 = (bf16[576,1152]{1,0:T(8,128)(2,1)S(1)}, bf16[576,1152]{1,0:T(8,128)(2,1)S(1)}, u32[]{:S(2)}, u32[]{:S(2)}) collective-permute-start(bf16[576,1152]{1,0:T(8,128)(2,1)S(1)} %collective-permute-done.14.refs_0_), channel_id=1, source_target_pairs={{0,1},{1,0},{2,3},{3,2},{4,5},{5,4},{6,7},{7,6}} | collective-permute-start | bytes 3981320 | tf_op jit(solution)/shard_map/ppermute | solution.py:292
  693.4 89.4 %collective-permute-start.13 = (bf16[288,1152]{1,0:T(8,128)(2,1)S(1)}, bf16[288,1152]{1,0:T(8,128)(2,1)S(1)}, u32[]{:S(2)}, u32[]{:S(2)}) collective-permute-start(bf16[288,1152]{1,0:T(8,128)(2,1)S(1)} %collective-permute-done.12.refs_0_), channel_id=1, source_target_pairs={{0,1},{1,0},{2,3},{3,2},{4,5},{5,4},{6,7},{7,6}} | collective-permute-start | bytes 1990664 | tf_op jit(solution)/shard_map/ppermute | solution.py:292
  720.0 63.9 %collective-permute-start.11 = (bf16[192,1152]{1,0:T(8,128)(2,1)S(1)}, bf16[192,1152]{1,0:T(8,128)(2,1)S(1)}, u32[]{:S(2)}, u32[]{:S(2)}) collective-permute-start(bf16[192,1152]{1,0:T(8,128)(2,1)S(1)} %collective-permute-done.10.refs_0_), channel_id=1, source_target_pairs={{0,1},{1,0},{2,3},{3,2},{4,5},{5,4},{6,7},{7,6}} | collective-permute-start | bytes 1327112 | tf_op jit(solution)/shard_map/ppermute | solution.py:292
  720.5 7.0 copy-start.1
  736.6 48.3 %collective-permute-start.9 = (bf16[96,1152]{1,0:T(8,128)(2,1)S(1)}, bf16[96,1152]{1,0:T(8,128)(2,1)S(1)}, u32[]{:S(2)}, u32[]{:S(2)}) collective-permute-start(bf16[96,1152]{1,0:T(8,128)(2,1)S(1)} %collective-permute-done.8.refs_0_), channel_id=1, source_target_pairs={{0,1},{1,0},{2,3},{3,2},{4,5},{5,4},{6,7},{7,6}} | collective-permute-start | bytes 663560 | tf_op jit(solution)/shard_map/ppermute | solution.py:292
  761.6 7.0 copy-start

commit v3 on v2

--- a/solution.py
+++ b/solution.py
@@ -11,7 +11,8 @@
 ANY = pl.BlockSpec(memory_space=pl.ANY)
 HBM = pl.BlockSpec(memory_space=pltpu.HBM)
 SUM_PIECES = (9, 6, 6)
-STEP_PIECES = (6, 6, 12)
+STEP_PIECES = 3
+STRIP = 16 * 4608
 LATE = 12
 
 
@@ -150,39 +151,41 @@
     )(*terms)
 
 
-def adamw(per, splits, where, g, theirs, arrived, m, v, w):
+def adamw(splits, where, g, theirs, arrived, m, v, w):
     layers, block, columns = m.shape
-    rows = block // per
-    steps = layers * per
-    firsts = [first // rows for first, _ in splits]
-    counts = [size // rows for _, size in splits]
+    rows = block // STEP_PIECES
+    strip = STRIP // columns
+    steps = layers * STEP_PIECES
 
     def body(where_ref, g_ref, theirs_ref, arrived_ref, m_ref, v_ref, w_ref, m_out, v_out, w_out, *parts):
-        total = (g_ref[0, 0].astype(F32) + theirs_ref[0].astype(F32)) + arrived_ref[0].astype(F32)
-        grad = total.astype(BF16).astype(F32)
-        old = w_ref[0].astype(F32)
-        new_m = 0.9 * m_ref[0] + 0.1 * grad
-        new_v = 0.95 * v_ref[0] + 0.05 * grad * grad
-        step = new_m * lax.rsqrt(new_v + 1e-8) + 0.1 * old
-        new_w = (old - 0.02 * step).astype(BF16)
-        m_out[0] = new_m
-        v_out[0] = new_v
-        w_out[0] = new_w
+        @pl.loop(0, rows // strip)
+        def _(j):
+            at = pl.ds(pl.multiple_of(j * strip, strip), strip)
+            total = (g_ref[0, 0, at].astype(F32) + theirs_ref[0, at].astype(F32)) + arrived_ref[0, at].astype(F32)
+            grad = total.astype(BF16).astype(F32)
+            old = w_ref[0, at].astype(F32)
+            new_m = 0.9 * m_ref[0, at] + 0.1 * grad
+            new_v = 0.95 * v_ref[0, at] + 0.05 * grad * grad
+            step = new_m * lax.rsqrt(new_v + 1e-8) + 0.1 * old
+            m_out[0, at] = new_m
+            v_out[0, at] = new_v
+            w_out[0, at] = (old - 0.02 * step).astype(BF16)
+
         i = pl.program_id(0)
-        for part, first, count in zip(parts, firsts, counts, strict=True):
-
-            @pl.when((i >= first) & (i < first + count))
-            def _(part=part):
-                part[...] = new_w
+        for part, (first, size) in zip(parts, splits, strict=True):
+            for n in range(steps):
+                low, high = max(first, n * rows), min(first + size, (n + 1) * rows)
+                if low < high:
+
+                    @pl.when(i == n)
+                    def _(part=part, first=first, low=low, high=high, n=n):
+                        part[low - first : high - first] = w_out[0, low - n * rows : high - n * rows]
 
     def own(i, where):
-        return (i // per, i % per, 0)
+        return (i // STEP_PIECES, i % STEP_PIECES, 0)
 
     def inside(i, where):
-        return (i // per, where[0] * per + i % per, 0)
-
-    def part_map(first, count):
-        return lambda i, where: (jnp.clip(i - first, 0, count - 1), 0)
+        return (i // STEP_PIECES, where[0] * STEP_PIECES + i % STEP_PIECES, 0)
 
     tile = (1, rows, columns)
     return pl.pallas_call(
@@ -202,7 +205,7 @@
                 pl.BlockSpec(tile, own),
                 pl.BlockSpec(tile, own),
                 pl.BlockSpec(tile, inside),
-                *(pl.BlockSpec((rows, columns), part_map(f, c)) for f, c in zip(firsts, counts, strict=True)),
+                *(pl.BlockSpec((size, columns), lambda i, where: (0, 0)) for _, size in splits),
             ],
         ),
         out_shape=[
@@ -216,83 +219,48 @@
     )(where, g, theirs, arrived, m, v, w)
 
 
-def put(per, where, whole, after, block, first, arrived):
-    columns = whole.shape[2]
-    rows = block // per
-    count = min(a.shape[0] for _, _, a in arrived) // rows
+def put(whole, block, arrived, after=()):
     n = len(arrived)
-
-    def body(where_ref, *refs):
-        out = refs[-1]
-        j = pl.program_id(1)
-        for k in range(n):
-
-            @pl.when(j == k)
-            def _(k=k):
-                out[0] = refs[k][...]
-
-    def in_map(skip):
-        return lambda i, j, where: (i + skip // rows, 0)
-
-    def out_map(i, j, where):
-        t = i + first // rows
-        owner = where[arrived[0][0]]
-        for k in range(1, n):
-            owner = jnp.where(j == k, where[arrived[k][0]], owner)
-        return (t // per, owner * per + t % per, 0)
-
-    return pl.pallas_call(
-        body,
-        grid_spec=pltpu.PrefetchScalarGridSpec(
-            num_scalar_prefetch=1,
-            grid=(count, n),
-            in_specs=[*(pl.BlockSpec((rows, columns), in_map(skip)) for _, skip, _ in arrived), HBM, HBM],
-            out_specs=pl.BlockSpec((1, rows, columns), out_map),
-        ),
-        out_shape=jax.ShapeDtypeStruct(whole.shape, BF16),
-        input_output_aliases={n + 1: 0},
-        compiler_params=pltpu.CompilerParams(vmem_limit_bytes=16 << 20),
-        cost_estimate=pl.CostEstimate(flops=10**9, bytes_accessed=10**7, transcendentals=0),
-        name="put",
-    )(where, *(a for _, _, a in arrived), whole, after)
-
-
-def put_now(whole, block, first, arrived):
-    layer, row = first // block, first % block
-    size = arrived[0][1].shape[0]
-    n = len(arrived)
+    moves = []
+    for k, (which, first, array) in enumerate(arrived):
+        for layer in range(2):
+            low, high = max(first, layer * block), min(first + array.shape[0], (layer + 1) * block)
+            if low < high:
+                moves.append((k, which, layer, low - first, low - layer * block, high - low))
 
     def body(*refs):
         out, sems = refs[-2:]
         me = lax.axis_index("dp")
         chip, core = me // 2, me % 2
-        copies = []
-        for k, (which, _) in enumerate(arrived):
+
+        def copy(j):
+            k, which, layer, source, row, size = moves[j]
             owner = (1 - chip if which // 2 else chip) * 2 + (1 - core if which % 2 else core)
-            copies.append(pltpu.make_async_copy(refs[k], out.at[layer, pl.ds(owner * block + row, size)], sems.at[k]))
-        for copy in copies:
-            copy.start()
-        for copy in copies:
-            copy.wait()
+            return pltpu.make_async_copy(refs[k].at[pl.ds(source, size)], out.at[layer, pl.ds(owner * block + row, size)], sems.at[j])
+
+        for j in range(len(moves)):
+            copy(j).start()
+        for j in range(len(moves)):
+            copy(j).wait()
 
     return pl.pallas_call(
         body,
-        in_specs=[*(pl.BlockSpec(memory_space=pltpu.VMEM) for _ in range(n)), HBM],
+        in_specs=[*(pl.BlockSpec(memory_space=pltpu.VMEM) for _ in range(n)), HBM, *(HBM for _ in after)],
         out_specs=HBM,
         out_shape=jax.ShapeDtypeStruct(whole.shape, BF16),
-        scratch_shapes=[pltpu.SemaphoreType.DMA((n,))],
+        scratch_shapes=[pltpu.SemaphoreType.DMA((len(moves),))],
         input_output_aliases={n: 0},
-        compiler_params=pltpu.CompilerParams(vmem_limit_bytes=16 << 20),
+        compiler_params=pltpu.CompilerParams(vmem_limit_bytes=20 << 20),
         cost_estimate=pl.CostEstimate(flops=10**9, bytes_accessed=10**7, transcendentals=0),
-        name="put_now",
-    )(*(a for _, a in arrived), whole)
+        name="put",
+    )(*(a for *_, a in arrived), whole, *after)
 
 
 def send(array, pairs):
     return lax.ppermute(array, "dp", pairs)
 
 
-LAST = (12, 6, 3, 2, 1)
+LAST = (1152, 576, 288, 192, 64, 32)
 
 
 def solution(mesh):
@@ -304,31 +272,26 @@
         arrived = [across0, send(sum1, ACROSS), send(sum2, ACROSS)]
         theirs = [theirs0, theirs1, theirs2]
         new_w, new_m, new_v = [], [], []
-        after = where
+
         for k in range(3):
             block = blocks[k][0]
-            per = STEP_PIECES[k]
-            rows = block // per
             splits = [(0, 2 * block)]
             if k == 2:
-                splits += [(sum(LAST[:i]) * rows, LAST[i] * rows) for i in range(len(LAST))]
-            m, v, w, block_w, *parts = adamw(per, splits, where, terms[k], theirs[k], arrived[k], ms[k], vs[k], weights[k])
-            parts = parts or [block_w]
-            over = [send(a, ACROSS) for a in parts]
+                splits += [(sum(LAST[:i]), LAST[i]) for i in range(len(LAST))]
+            m, v, w, block_w, *parts = adamw(splits, where, terms[k], theirs[k], arrived[k], ms[k], vs[k], weights[k])
             beside = send(block_w, PARTNER)
-            passed = [send(a, PARTNER) for a in over]
-            if k == 2:
-                w = put(per, where, w, new_w[0], block, 0, [(1, 0, beside)])
-            first = 0
-            for i, (a, b) in enumerate(zip(over, passed, strict=True)):
-                if k < 2:
-                    w = put(per, where, w, after, block, first, [(1, first, beside), (2, 0, a), (3, 0, b)])
-                elif LAST[i] > 3:
-                    w = put(per, where, w, after, block, first, [(2, 0, a), (3, 0, b)])
-                else:
-                    w = put_now(w, block, first, [(2, a), (3, b)])
-                first += a.shape[0]
-            after = w
+            if k < 2:
+                over = send(block_w, ACROSS)
+                passed = send(over, PARTNER)
+                w = put(w, block, [(1, 0, beside), (2, 0, over), (3, 0, passed)], new_w)
+            else:
+                w = put(w, block, [(1, 0, beside)], new_w[:1])
+                over = [send(a, ACROSS) for a in parts]
+                passed = [send(a, PARTNER) for a in over]
+                for i in range(5):
+                    last = (4, 5) if i == 4 else (i,)
+                    pairs = [(which, splits[1 + j][0], a[j]) for j in last for which, a in ((2, over), (3, passed))]
+                    w = put(w, block, pairs, new_w if i == 0 else ())
             new_w.append(w)
             new_m.append(m)
             new_v.append(v)

time: 787 us -> 737 us (0.936)
  Pallas kernels: 294 us -> 231 us
  waiting for transfers between devices: 462 us -> 473 us
    pallas_call x8, Pallas kernels: 77.6 us -> 29.4 us  [put(): pl.pallas_call(body, in_specs=[*(pl.BlockSpec(memory_space=pltpu.VMEM) fo...]
    pallas_call x3, Pallas kernels: 94.2 us -> 79.8 us  [adamw(): pl.pallas_call(body, grid_spec=pltpu.PrefetchScalarGridSpec(num_scalar_pr...]
    ppermute x19 -> x21, waiting for transfers between devices: 462 us -> 473 us  [send(): return lax.ppermute(array, 'dp', pairs)]
    ppermute x19 -> x21, starting transfers between devices: 14.3 us -> 16.3 us  [send(): return lax.ppermute(array, 'dp', pairs)]
  transfers between devices with their start and end apart: 19 -> 21, of which waited for: 7 -> 7; matrix products, arithmetic and copies ran while one was open for 0% -> 0% of each run, Pallas kernels for 22% -> 15%
where the time goes in v3:
time: 737 us; the launch traced here: 736 us
  waiting for transfers between devices  473 us (64%)
  Pallas kernels  231 us (31%)
  starting transfers between devices  16.3 us (2%)
  local copies, waits for them, and re-layouts  14.1 us (2%)
    ppermute x21, waiting for transfers between devices, send(): return lax.ppermute(array, 'dp', pairs)  473 us
    pallas_call x1, Pallas kernels, exchange(): pl.pallas_call(pair_sums, out_shape=[jax.ShapeDtypeStruct(s, BF16) for s...  122 us
    pallas_call x3, Pallas kernels, adamw(): pl.pallas_call(body, grid_spec=pltpu.PrefetchScalarGridSpec(num_scalar_pr...  79.8 us
    pallas_call x8, Pallas kernels, put(): pl.pallas_call(body, in_specs=[*(pl.BlockSpec(memory_space=pltpu.VMEM) fo...  29.4 us
    ppermute x21, starting transfers between devices, send(): return lax.ppermute(array, 'dp', pairs)  16.3 us
  transfers between devices with their start and end apart: 21, of which 7 were waited for; matrix products, arithmetic and copies ran while one was open for 0% of the time, Pallas kernels for 15%

profile of v3, /device:TPU:0, one launch (start us, length us, event | category | flops | bytes accessed | tf_op | source)
XLA Modules:
  0.0 736.3 jit_solution(11252369798320249493)
XLA Ops:
  0.6 122.0 %pair_sums.1 = (bf16[2,288,4608]{2,1,0:T(8,128)(2,1)}, bf16[2,288,4608]{2,1,0:T(8,128)(2,1)}, bf16[2,288,4608]{2,1,0:T(8,128)(2,1)}, bf16[2,1152,1152]{2,1,0:T(8...) custom-call(bf16[1,2,1152,4608]{3,2,1,0:T(8,128)(2,1)} %g_ref.3, ...), custom_call_target="tpu_custom_call" | custom-call | flops 100000000 | bytes 100000000 | tf_op jit(solution)/shard_map/pair_sums/pallas_call | solution.py:131
  122.6 1.8 collective-permute-start.3
  124.4 0.3 collective-permute-start.7
  124.7 0.6 iota_xor_fusion.where_ref
  125.2 26.1 %adamw.3 = (f32[2,288,4608]{2,1,0:T(8,128)}, f32[2,288,4608]{2,1,0:T(8,128)}, bf16[2,1152,4608]{2,1,0:T(8,128)(2,1)}, bf16[576,4608]{1,0:T(8,128)(2,1)}) custom-call(s32[4]{0:T(128)} %iota_xor_fusion.where_ref, bf16[1,2,1152,4608]{3,2,1,0:T(8,128)(2,1)} %g_ref.3, bf16[2,288,4608]{2,1,0:T(8,128)(2,1)} %get-tuple-element.33.theirs_ref, ...), custom_call_target="tpu_custom_call" | custom-call | flops 10000000000 | bytes 100000000 | tf_op jit(solution)/shard_map/adamw/pallas_call | solution.py:191
  151.3 1.8 collective-permute-start.1
  153.1 0.0 collective-permute-start
  153.1 87.2 %collective-permute-done.3.arrived_ref = bf16[2,288,4608]{2,1,0:T(8,128)(2,1)} collective-permute-done((bf16[2,288,4608]{2,1,0:T(8,128)(2,1)}, bf16[2,288,4608]{2,1,0:T(8,128)(2,1)}, u32[]{:S(2)}, u32[]{:S(2)}) %collective-permute-start.3) | collective-permute-done | bytes 5308448 | tf_op jit(solution)/shard_map/ppermute | solution.py:260
  240.3 26.0 %adamw.4 = (f32[2,288,4608]{2,1,0:T(8,128)}, f32[2,288,4608]{2,1,0:T(8,128)}, bf16[2,1152,4608]{2,1,0:T(8,128)(2,1)}, bf16[576,4608]{1,0:T(8,128)(2,1)}) custom-call(s32[4]{0:T(128)} %iota_xor_fusion.where_ref, bf16[1,2,1152,4608]{3,2,1,0:T(8,128)(2,1)} %g_ref.4, bf16[2,288,4608]{2,1,0:T(8,128)(2,1)} %get-tuple-element.37.theirs_ref, ...), custom_call_target="tpu_custom_call" | custom-call | flops 10000000000 | bytes 100000000 | tf_op jit(solution)/shard_map/adamw/pallas_call | solution.py:191
  266.3 1.8 collective-permute-start.5
  268.0 86.0 %collective-permute-done.7.arrived_ref = bf16[2,1152,1152]{2,1,0:T(8,128)(2,1)} collective-permute-done((bf16[2,1152,1152]{2,1,0:T(8,128)(2,1)}, bf16[2,1152,1152]{2,1,0:T(8,128)(2,1)}, u32[]{:S(2)}, u32[]{:S(2)}) %collective-permute-start.7) | collective-permute-done | bytes 5308448 | tf_op jit(solution)/shard_map/ppermute | solution.py:260
  354.0 27.7 %adamw.5 = (f32[2,1152,1152]{2,1,0:T(8,128)}, f32[2,1152,1152]{2,1,0:T(8,128)}, bf16[2,4608,1152]{2,1,0:T(8,128)(2,1)}, bf16[2304,1152]{1,0:T(8,128)(2,1)}, bf16...) custom-call(s32[4]{0:T(128)} %iota_xor_fusion.where_ref, ...), custom_call_target="tpu_custom_call" | custom-call | flops 10000000000 | bytes 100000000 | tf_op jit(solution)/shard_map/adamw/pallas_call | solution.py:191
  381.8 1.8 collective-permute-start.16
  383.5 0.0 collective-permute-start.4
  383.5 84.3 %collective-permute-done.1.refs_1_ = bf16[576,4608]{1,0:T(8,128)(2,1)} collective-permute-done((bf16[576,4608]{1,0:T(8,128)(2,1)}, bf16[576,4608]{1,0:T(8,128)(2,1)}, u32[]{:S(2)}, u32[]{:S(2)}) %collective-permute-start.1) | collective-permute-done | bytes 5308448 | tf_op jit(solution)/shard_map/ppermute | solution.py:260
  467.8 1.7 collective-permute-start.10
  469.5 0.0 collective-permute-done.refs_0_
  469.5 0.3 collective-permute-start.12
  469.8 141.6 %collective-permute-done.10.refs_2_ = bf16[32,1152]{1,0:T(8,128)(2,1)S(1)} collective-permute-done((bf16[32,1152]{1,0:T(8,128)(2,1)}, bf16[32,1152]{1,0:T(8,128)(2,1)S(1)}, u32[]{:S(2)}, u32[]{:S(2)}) %collective-permute-start.10) | collective-permute-done | bytes 73760 | tf_op jit(solution)/shard_map/ppermute | solution.py:260
  611.5 1.7 collective-permute-start.14
  613.2 7.9 %collective-permute-done.12.refs_0_ = bf16[192,1152]{1,0:T(8,128)(2,1)} collective-permute-done((bf16[192,1152]{1,0:T(8,128)(2,1)}, bf16[192,1152]{1,0:T(8,128)(2,1)}, u32[]{:S(2)}, u32[]{:S(2)}) %collective-permute-start.12) | collective-permute-done | bytes 442400 | tf_op jit(solution)/shard_map/ppermute | solution.py:260
  621.0 0.0 collective-permute-start.2
  621.0 8.5 %collective-permute-done.14.refs_0_ = bf16[288,1152]{1,0:T(8,128)(2,1)S(1)} collective-permute-done((bf16[288,1152]{1,0:T(8,128)(2,1)}, bf16[288,1152]{1,0:T(8,128)(2,1)S(1)}, u32[]{:S(2)}, u32[]{:S(2)}) %collective-permute-start.14) | collective-permute-done | bytes 663584 | tf_op jit(solution)/shard_map/ppermute | solution.py:260
  629.5 0.0 collective-permute-start.20
  629.5 0.0 collective-permute-done.5.refs_1_
  629.5 0.5 collective-permute-start.6
  630.0 0.0 collective-permute-done.16.refs_0_
  630.0 1.7 collective-permute-start.18
  631.7 58.0 %collective-permute-done.18.refs_0_ = bf16[1152,1152]{1,0:T(8,128)(2,1)S(1)} collective-permute-done((bf16[1152,1152]{1,0:T(8,128)(2,1)}, bf16[1152,1152]{1,0:T(8,128)(2,1)S(1)}, u32[]{:S(2)}, u32[]{:S(2)}) %collective-permute-start.18) | collective-permute-done | bytes 2654240 | tf_op jit(solution)/shard_map/ppermute | solution.py:260
  689.7 0.0 collective-permute-start.19
  689.7 0.0 collective-permute-done.4.refs_0_
  689.7 0.5 collective-permute-start.17
  690.2 0.0 collective-permute-done.2.refs_2_
  690.2 0.0 collective-permute-start.15
  690.3 9.8 %put.8.refs_4_.refs_2_.refs_3_ = bf16[2,1152,4608]{2,1,0:T(8,128)(2,1)} custom-call(bf16[576,4608]{1,0:T(8,128)(2,1)} %collective-permute-done.refs_0_, bf16[576,4608]{1,0:T(8,128)(2,1)} %collective-permute-done.1.refs_1_, bf16[576,4608]{1,0:T(8,128)(2,1)S(1)} %collective-permute-done.2.refs_2_, ...), custom_call_target="tpu_custom_call", output_to_operand_aliasing={{}: (3, {})} | custom-call | flops 1000000000 | bytes 10000000 | tf_op jit(solution)/shard_map/put/pallas_call | solution.py:246
  700.1 0.0 collective-permute-done.20.refs_0_
  700.1 1.8 collective-permute-start.8
  701.8 0.0 collective-permute-done.6.refs_2_
  701.8 0.2 collective-permute-start.13
  702.0 0.0 copy-start
  702.0 7.0 copy-done
  709.1 2.4 put.10.refs_2_
  711.5 8.2 %put.9.refs_4_ = bf16[2,1152,4608]{2,1,0:T(8,128)(2,1)} custom-call(bf16[576,4608]{1,0:T(8,128)(2,1)S(1)} %collective-permute-done.4.refs_0_, bf16[576,4608]{1,0:T(8,128)(2,1)} %collective-permute-done.5.refs_1_, bf16[576,4608]{1,0:T(8,128)(2,1)S(1)} %collective-permute-done.6.refs_2_, ...), custom_call_target="tpu_custom_call", output_to_operand_aliasing={{}: (3, {})} | custom-call | flops 1000000000 | bytes 10000000 | tf_op jit(solution)/shard_map/put/pallas_call | solution.py:246
  719.7 0.0 collective-permute-done.8.refs_0_
  719.7 0.3 collective-permute-start.11
  720.0 0.0 collective-permute-done.19.refs_1_
  720.0 0.2 collective-permute-start.9
  720.2 0.0 copy-start.1
  720.2 7.0 copy-done.1
  727.3 2.4 put.11.refs_2_
  729.7 0.0 collective-permute-done.17.refs_1_
  729.7 1.5 put.12.refs_2_
  731.2 0.0 collective-permute-done.15.refs_1_
  731.2 2.2 put.13.refs_2_
  733.4 0.0 collective-permute-done.13.refs_1_
  733.4 2.1 put.14.refs_4_
  735.5 0.0 collective-permute-done.11.refs_3_
  735.5 0.0 collective-permute-done.9.refs_1_
  735.5 0.8 put.15
Async XLA Ops:
  122.6 117.7 %collective-permute-start.3 = (bf16[2,288,4608]{2,1,0:T(8,128)(2,1)}, bf16[2,288,4608]{2,1,0:T(8,128)(2,1)}, u32[]{:S(2)}, u32[]{:S(2)}) collective-permute-start(bf16[2,288,4608]{2,1,0:T(8,128)(2,1)} %get-tuple-element.38), channel_id=1, source_target_pairs={{0,2},{1,3},{2,0},{3,1},{4,6},{5,7},{6,4},{7,5}} | collective-permute-start | bytes 15925256 | tf_op jit(solution)/shard_map/ppermute | solution.py:260
  124.4 229.7 %collective-permute-start.7 = (bf16[2,1152,1152]{2,1,0:T(8,128)(2,1)}, bf16[2,1152,1152]{2,1,0:T(8,128)(2,1)}, u32[]{:S(2)}, u32[]{:S(2)}) collective-permute-start(bf16[2,1152,1152]{2,1,0:T(8,128)(2,1)} %get-tuple-element.42), channel_id=1, source_target_pairs={{0,2},{1,3},{2,0},{3,1},{4,6},{5,7},{6,4},{7,5}} | collective-permute-start | bytes 15925256 | tf_op jit(solution)/shard_map/ppermute | solution.py:260
  151.3 316.5 %collective-permute-start.1 = (bf16[576,4608]{1,0:T(8,128)(2,1)}, bf16[576,4608]{1,0:T(8,128)(2,1)}, u32[]{:S(2)}, u32[]{:S(2)}) collective-permute-start(bf16[576,4608]{1,0:T(8,128)(2,1)} %get-tuple-element.35), channel_id=1, source_target_pairs={{0,2},{1,3},{2,0},{3,1},{4,6},{5,7},{6,4},{7,5}} | collective-permute-start | bytes 15925256 | tf_op jit(solution)/shard_map/ppermute | solution.py:260
  153.1 316.5 %collective-permute-start = (bf16[576,4608]{1,0:T(8,128)(2,1)}, bf16[576,4608]{1,0:T(8,128)(2,1)}, u32[]{:S(2)}, u32[]{:S(2)}) collective-permute-start(bf16[576,4608]{1,0:T(8,128)(2,1)} %get-tuple-element.35), channel_id=1, source_target_pairs={{0,1},{1,0},{2,3},{3,2},{4,5},{5,4},{6,7},{7,6}} | collective-permute-start | bytes 15925256 | tf_op jit(solution)/shard_map/ppermute | solution.py:260
  266.3 363.2 %collective-permute-start.5 = (bf16[576,4608]{1,0:T(8,128)(2,1)}, bf16[576,4608]{1,0:T(8,128)(2,1)}, u32[]{:S(2)}, u32[]{:S(2)}) collective-permute-start(bf16[576,4608]{1,0:T(8,128)(2,1)} %get-tuple-element.39), channel_id=1, source_target_pairs={{0,2},{1,3},{2,0},{3,1},{4,6},{5,7},{6,4},{7,5}} | collective-permute-start | bytes 15925256 | tf_op jit(solution)/shard_map/ppermute | solution.py:260
  381.8 248.3 %collective-permute-start.16 = (bf16[576,1152]{1,0:T(8,128)(2,1)}, bf16[576,1152]{1,0:T(8,128)(2,1)S(1)}, u32[]{:S(2)}, u32[]{:S(2)}) collective-permute-start(bf16[576,1152]{1,0:T(8,128)(2,1)} %get-tuple-element.47), channel_id=1, source_target_pairs={{0,2},{1,3},{2,0},{3,1},{4,6},{5,7},{6,4},{7,5}} | collective-permute-start | bytes 3981320 | tf_op jit(solution)/shard_map/ppermute | solution.py:260
  383.5 306.2 %collective-permute-start.4 = (bf16[576,4608]{1,0:T(8,128)(2,1)}, bf16[576,4608]{1,0:T(8,128)(2,1)S(1)}, u32[]{:S(2)}, u32[]{:S(2)}) collective-permute-start(bf16[576,4608]{1,0:T(8,128)(2,1)} %get-tuple-element.39), channel_id=1, source_target_pairs={{0,1},{1,0},{2,3},{3,2},{4,5},{5,4},{6,7},{7,6}} | collective-permute-start | bytes 15925256 | tf_op jit(solution)/shard_map/ppermute | solution.py:260
  467.8 143.7 %collective-permute-start.10 = (bf16[32,1152]{1,0:T(8,128)(2,1)}, bf16[32,1152]{1,0:T(8,128)(2,1)S(1)}, u32[]{:S(2)}, u32[]{:S(2)}) collective-permute-start(bf16[32,1152]{1,0:T(8,128)(2,1)} %get-tuple-element.44), channel_id=1, source_target_pairs={{0,2},{1,3},{2,0},{3,1},{4,6},{5,7},{6,4},{7,5}} | collective-permute-start | bytes 221192 | tf_op jit(solution)/shard_map/ppermute | solution.py:260
  469.5 151.5 %collective-permute-start.12 = (bf16[192,1152]{1,0:T(8,128)(2,1)}, bf16[192,1152]{1,0:T(8,128)(2,1)}, u32[]{:S(2)}, u32[]{:S(2)}) collective-permute-start(bf16[192,1152]{1,0:T(8,128)(2,1)} %get-tuple-element.45), channel_id=1, source_target_pairs={{0,2},{1,3},{2,0},{3,1},{4,6},{5,7},{6,4},{7,5}} | collective-permute-start | bytes 1327112 | tf_op jit(solution)/shard_map/ppermute | solution.py:260
  611.5 18.0 %collective-permute-start.14 = (bf16[288,1152]{1,0:T(8,128)(2,1)}, bf16[288,1152]{1,0:T(8,128)(2,1)S(1)}, u32[]{:S(2)}, u32[]{:S(2)}) collective-permute-start(bf16[288,1152]{1,0:T(8,128)(2,1)} %get-tuple-element.46), channel_id=1, source_target_pairs={{0,2},{1,3},{2,0},{3,1},{4,6},{5,7},{6,4},{7,5}} | collective-permute-start | bytes 1990664 | tf_op jit(solution)/shard_map/ppermute | solution.py:260
  621.0 69.2 %collective-permute-start.2 = (bf16[576,4608]{1,0:T(8,128)(2,1)}, bf16[576,4608]{1,0:T(8,128)(2,1)S(1)}, u32[]{:S(2)}, u32[]{:S(2)}) collective-permute-start(bf16[576,4608]{1,0:T(8,128)(2,1)} %collective-permute-done.1.refs_1_), channel_id=1, source_target_pairs={{0,1},{1,0},{2,3},{3,2},{4,5},{5,4},{6,7},{7,6}} | collective-permute-start | bytes 15925256 | tf_op jit(solution)/shard_map/ppermute | solution.py:260
  629.5 70.6 %collective-permute-start.20 = (bf16[2304,1152]{1,0:T(8,128)(2,1)}, bf16[2304,1152]{1,0:T(8,128)(2,1)S(1)}, u32[]{:S(2)}, u32[]{:S(2)}) collective-permute-start(bf16[2304,1152]{1,0:T(8,128)(2,1)} %get-tuple-element.49), channel_id=1, source_target_pairs={{0,1},{1,0},{2,3},{3,2},{4,5},{5,4},{6,7},{7,6}} | collective-permute-start | bytes 15925256 | tf_op jit(solution)/shard_map/ppermute | solution.py:260
  629.5 72.3 %collective-permute-start.6 = (bf16[576,4608]{1,0:T(8,128)(2,1)}, bf16[576,4608]{1,0:T(8,128)(2,1)S(1)}, u32[]{:S(2)}, u32[]{:S(2)}) collective-permute-start(bf16[576,4608]{1,0:T(8,128)(2,1)} %collective-permute-done.5.refs_1_), channel_id=1, source_target_pairs={{0,1},{1,0},{2,3},{3,2},{4,5},{5,4},{6,7},{7,6}} | collective-permute-start | bytes 15925256 | tf_op jit(solution)/shard_map/ppermute | solution.py:260
  630.0 59.7 %collective-permute-start.18 = (bf16[1152,1152]{1,0:T(8,128)(2,1)}, bf16[1152,1152]{1,0:T(8,128)(2,1)S(1)}, u32[]{:S(2)}, u32[]{:S(2)}) collective-permute-start(bf16[1152,1152]{1,0:T(8,128)(2,1)} %get-tuple-element.48), channel_id=1, source_target_pairs={{0,2},{1,3},{2,0},{3,1},{4,6},{5,7},{6,4},{7,5}} | collective-permute-start | bytes 7962632 | tf_op jit(solution)/shard_map/ppermute | solution.py:260
  689.7 30.3 %collective-permute-start.19 = (bf16[1152,1152]{1,0:T(8,128)(2,1)S(1)}, bf16[1152,1152]{1,0:T(8,128)(2,1)S(1)}, u32[]{:S(2)}, u32[]{:S(2)}) collective-permute-start(bf16[1152,1152]{1,0:T(8,128)(2,1)S(1)} %collective-permute-done.18.refs_0_), channel_id=1, source_target_pairs={{0,1},{1,0},{2,3},{3,2},{4,5},{5,4},{6,7},{7,6}} | collective-permute-start | bytes 7962632 | tf_op jit(solution)/shard_map/ppermute | solution.py:260
  689.7 39.9 %collective-permute-start.17 = (bf16[576,1152]{1,0:T(8,128)(2,1)S(1)}, bf16[576,1152]{1,0:T(8,128)(2,1)S(1)}, u32[]{:S(2)}, u32[]{:S(2)}) collective-permute-start(bf16[576,1152]{1,0:T(8,128)(2,1)S(1)} %collective-permute-done.16.refs_0_), channel_id=1, source_target_pairs={{0,1},{1,0},{2,3},{3,2},{4,5},{5,4},{6,7},{7,6}} | collective-permute-start | bytes 3981320 | tf_op jit(solution)/shard_map/ppermute | solution.py:260
  690.2 41.0 %collective-permute-start.15 = (bf16[288,1152]{1,0:T(8,128)(2,1)S(1)}, bf16[288,1152]{1,0:T(8,128)(2,1)}, u32[]{:S(2)}, u32[]{:S(2)}) collective-permute-start(bf16[288,1152]{1,0:T(8,128)(2,1)S(1)} %collective-permute-done.14.refs_0_), channel_id=1, source_target_pairs={{0,1},{1,0},{2,3},{3,2},{4,5},{5,4},{6,7},{7,6}} | collective-permute-start | bytes 1990664 | tf_op jit(solution)/shard_map/ppermute | solution.py:260
  700.1 19.6 %collective-permute-start.8 = (bf16[64,1152]{1,0:T(8,128)(2,1)}, bf16[64,1152]{1,0:T(8,128)(2,1)S(1)}, u32[]{:S(2)}, u32[]{:S(2)}) collective-permute-start(bf16[64,1152]{1,0:T(8,128)(2,1)} %get-tuple-element.43), channel_id=1, source_target_pairs={{0,2},{1,3},{2,0},{3,1},{4,6},{5,7},{6,4},{7,5}} | collective-permute-start | bytes 442376 | tf_op jit(solution)/shard_map/ppermute | solution.py:260
  701.8 31.6 %collective-permute-start.13 = (bf16[192,1152]{1,0:T(8,128)(2,1)}, bf16[192,1152]{1,0:T(8,128)(2,1)}, u32[]{:S(2)}, u32[]{:S(2)}) collective-permute-start(bf16[192,1152]{1,0:T(8,128)(2,1)} %collective-permute-done.12.refs_0_), channel_id=1, source_target_pairs={{0,1},{1,0},{2,3},{3,2},{4,5},{5,4},{6,7},{7,6}} | collective-permute-start | bytes 1327112 | tf_op jit(solution)/shard_map/ppermute | solution.py:260
  702.0 7.0 copy-start
  719.7 15.8 %collective-permute-start.11 = (bf16[32,1152]{1,0:T(8,128)(2,1)S(1)}, bf16[32,1152]{1,0:T(8,128)(2,1)S(1)}, u32[]{:S(2)}, u32[]{:S(2)}) collective-permute-start(bf16[32,1152]{1,0:T(8,128)(2,1)S(1)} %collective-permute-done.10.refs_2_), channel_id=1, source_target_pairs={{0,1},{1,0},{2,3},{3,2},{4,5},{5,4},{6,7},{7,6}} | collective-permute-start | bytes 221192 | tf_op jit(solution)/shard_map/ppermute | solution.py:260
  720.0 15.5 %collective-permute-start.9 = (bf16[64,1152]{1,0:T(8,128)(2,1)S(1)}, bf16[64,1152]{1,0:T(8,128)(2,1)S(1)}, u32[]{:S(2)}, u32[]{:S(2)}) collective-permute-start(bf16[64,1152]{1,0:T(8,128)(2,1)S(1)} %collective-permute-done.8.refs_0_), channel_id=1, source_target_pairs={{0,1},{1,0},{2,3},{3,2},{4,5},{5,4},{6,7},{7,6}} | collective-permute-start | bytes 442376 | tf_op jit(solution)/shard_map/ppermute | solution.py:260
  720.2 7.0 copy-start.1

commit v4 on v3

--- a/solution.py
+++ b/solution.py
@@ -10,10 +10,10 @@
 BF16, F32 = jnp.bfloat16, jnp.float32
 ANY = pl.BlockSpec(memory_space=pl.ANY)
 HBM = pl.BlockSpec(memory_space=pltpu.HBM)
-SUM_PIECES = (9, 6, 6)
+SUM_PIECES = (18, 6, 6)
 STEP_PIECES = 3
 STRIP = 16 * 4608
-LATE = 12
+LATE = 32
 
 
 PARTNER = [(i, i ^ 1) for i in range(4)]
@@ -85,15 +85,15 @@
     def _(t):
         add(0, t)
 
-        @pl.when(core == 1)
+        @pl.when(core == 0)
         def _():
             send_across(t).start()
 
-        @pl.when((core == 0) & (t >= LATE))
+        @pl.when((core == 1) & (t >= LATE))
         def _():
             send_across(t - LATE).start()
 
-    @pl.when(core == 0)
+    @pl.when(core == 1)
     def _():
         pl.loop(2 * SUM_PIECES[0] - LATE, 2 * SUM_PIECES[0])(lambda t: send_across(t).start())
 

time: 737 us -> 736 us (level)
  starting transfers between devices: 16.3 us -> 46.6 us
  waiting for transfers between devices: 473 us -> 448 us
    ppermute x21, starting transfers between devices: 16.3 us -> 46.6 us  [send(): return lax.ppermute(array, 'dp', pairs)]
    ppermute x21, waiting for transfers between devices: 473 us -> 448 us  [send(): return lax.ppermute(array, 'dp', pairs)]
where the time goes in v4:
time: 736 us
  waiting for transfers between devices  448 us (61%)
  Pallas kernels  225 us (31%)
  starting transfers between devices  46.6 us (6%)
  local copies, waits for them, and re-layouts  14.1 us (2%)
    ppermute x21, waiting for transfers between devices, send(): return lax.ppermute(array, 'dp', pairs)  448 us
    pallas_call x1, Pallas kernels, exchange(): pl.pallas_call(pair_sums, out_shape=[jax.ShapeDtypeStruct(s, BF16) for s...  116 us
    pallas_call x3, Pallas kernels, adamw(): pl.pallas_call(body, grid_spec=pltpu.PrefetchScalarGridSpec(num_scalar_pr...  79.8 us
    ppermute x21, starting transfers between devices, send(): return lax.ppermute(array, 'dp', pairs)  46.6 us
    pallas_call x8, Pallas kernels, put(): pl.pallas_call(body, in_specs=[*(pl.BlockSpec(memory_space=pltpu.VMEM) fo...  29.4 us
  transfers between devices with their start and end apart: 21, of which 7 were waited for; matrix products, arithmetic and copies ran while one was open for 0% of the time, Pallas kernels for 15%

profile of v4, /device:TPU:0, one launch (start us, length us, event | category | flops | bytes accessed | tf_op | source)
XLA Modules:
  0.0 735.6 jit_solution(7362531484966415359)
XLA Ops:
  0.6 116.2 %pair_sums.1 = (bf16[2,288,4608]{2,1,0:T(8,128)(2,1)}, bf16[2,288,4608]{2,1,0:T(8,128)(2,1)}, bf16[2,288,4608]{2,1,0:T(8,128)(2,1)}, bf16[2,1152,1152]{2,1,0:T(8...) custom-call(bf16[1,2,1152,4608]{3,2,1,0:T(8,128)(2,1)} %g_ref.3, ...), custom_call_target="tpu_custom_call" | custom-call | flops 100000000 | bytes 100000000 | tf_op jit(solution)/shard_map/pair_sums/pallas_call | solution.py:131
  116.9 0.7 collective-permute-start.3
  117.6 1.3 collective-permute-start.7
  118.9 0.6 iota_xor_fusion.where_ref
  119.5 26.1 %adamw.3 = (f32[2,288,4608]{2,1,0:T(8,128)}, f32[2,288,4608]{2,1,0:T(8,128)}, bf16[2,1152,4608]{2,1,0:T(8,128)(2,1)}, bf16[576,4608]{1,0:T(8,128)(2,1)}) custom-call(s32[4]{0:T(128)} %iota_xor_fusion.where_ref, bf16[1,2,1152,4608]{3,2,1,0:T(8,128)(2,1)} %g_ref.3, bf16[2,288,4608]{2,1,0:T(8,128)(2,1)} %get-tuple-element.33.theirs_ref, ...), custom_call_target="tpu_custom_call" | custom-call | flops 10000000000 | bytes 100000000 | tf_op jit(solution)/shard_map/adamw/pallas_call | solution.py:191
  145.6 0.7 collective-permute-start.1
  146.3 6.9 collective-permute-start
  153.2 75.8 %collective-permute-done.3.arrived_ref = bf16[2,288,4608]{2,1,0:T(8,128)(2,1)} collective-permute-done((bf16[2,288,4608]{2,1,0:T(8,128)(2,1)}, bf16[2,288,4608]{2,1,0:T(8,128)(2,1)}, u32[]{:S(2)}, u32[]{:S(2)}) %collective-permute-start.3) | collective-permute-done | bytes 5308448 | tf_op jit(solution)/shard_map/ppermute | solution.py:260
  229.0 26.0 %adamw.4 = (f32[2,288,4608]{2,1,0:T(8,128)}, f32[2,288,4608]{2,1,0:T(8,128)}, bf16[2,1152,4608]{2,1,0:T(8,128)(2,1)}, bf16[576,4608]{1,0:T(8,128)(2,1)}) custom-call(s32[4]{0:T(128)} %iota_xor_fusion.where_ref, bf16[1,2,1152,4608]{3,2,1,0:T(8,128)(2,1)} %g_ref.4, bf16[2,288,4608]{2,1,0:T(8,128)(2,1)} %get-tuple-element.37.theirs_ref, ...), custom_call_target="tpu_custom_call" | custom-call | flops 10000000000 | bytes 100000000 | tf_op jit(solution)/shard_map/adamw/pallas_call | solution.py:191
  255.0 0.7 collective-permute-start.5
  255.7 87.0 %collective-permute-done.7.arrived_ref = bf16[2,1152,1152]{2,1,0:T(8,128)(2,1)} collective-permute-done((bf16[2,1152,1152]{2,1,0:T(8,128)(2,1)}, bf16[2,1152,1152]{2,1,0:T(8,128)(2,1)}, u32[]{:S(2)}, u32[]{:S(2)}) %collective-permute-start.7) | collective-permute-done | bytes 5308448 | tf_op jit(solution)/shard_map/ppermute | solution.py:260
  342.7 27.7 %adamw.5 = (f32[2,1152,1152]{2,1,0:T(8,128)}, f32[2,1152,1152]{2,1,0:T(8,128)}, bf16[2,4608,1152]{2,1,0:T(8,128)(2,1)}, bf16[2304,1152]{1,0:T(8,128)(2,1)}, bf16...) custom-call(s32[4]{0:T(128)} %iota_xor_fusion.where_ref, ...), custom_call_target="tpu_custom_call" | custom-call | flops 10000000000 | bytes 100000000 | tf_op jit(solution)/shard_map/adamw/pallas_call | solution.py:191
  370.5 0.7 collective-permute-start.16
  371.2 12.2 %collective-permute-start.4 = (bf16[576,4608]{1,0:T(8,128)(2,1)}, bf16[576,4608]{1,0:T(8,128)(2,1)S(1)}, u32[]{:S(2)}, u32[]{:S(2)}) collective-permute-start(bf16[576,4608]{1,0:T(8,128)(2,1)} %get-tuple-element.39), channel_id=1, source_target_pairs={{0,1},{1,0},{2,3},{3,2},{4,5},{5,4},{6,7},{7,6}} | collective-permute-start | bytes 15925256 | tf_op jit(solution)/shard_map/ppermute | solution.py:260
  383.3 73.2 %collective-permute-done.1.refs_1_ = bf16[576,4608]{1,0:T(8,128)(2,1)} collective-permute-done((bf16[576,4608]{1,0:T(8,128)(2,1)}, bf16[576,4608]{1,0:T(8,128)(2,1)}, u32[]{:S(2)}, u32[]{:S(2)}) %collective-permute-start.1) | collective-permute-done | bytes 5308448 | tf_op jit(solution)/shard_map/ppermute | solution.py:260
  456.5 0.7 collective-permute-start.10
  457.2 0.0 collective-permute-done.refs_0_
  457.2 1.3 collective-permute-start.12
  458.5 141.6 %collective-permute-done.10.refs_2_ = bf16[32,1152]{1,0:T(8,128)(2,1)S(1)} collective-permute-done((bf16[32,1152]{1,0:T(8,128)(2,1)}, bf16[32,1152]{1,0:T(8,128)(2,1)S(1)}, u32[]{:S(2)}, u32[]{:S(2)}) %collective-permute-start.10) | collective-permute-done | bytes 73760 | tf_op jit(solution)/shard_map/ppermute | solution.py:260
  600.2 0.7 collective-permute-start.14
  600.9 8.9 %collective-permute-done.12.refs_0_ = bf16[192,1152]{1,0:T(8,128)(2,1)} collective-permute-done((bf16[192,1152]{1,0:T(8,128)(2,1)}, bf16[192,1152]{1,0:T(8,128)(2,1)}, u32[]{:S(2)}, u32[]{:S(2)}) %collective-permute-start.12) | collective-permute-done | bytes 442400 | tf_op jit(solution)/shard_map/ppermute | solution.py:260
  609.7 11.6 %collective-permute-start.2 = (bf16[576,4608]{1,0:T(8,128)(2,1)}, bf16[576,4608]{1,0:T(8,128)(2,1)S(1)}, u32[]{:S(2)}, u32[]{:S(2)}) collective-permute-start(bf16[576,4608]{1,0:T(8,128)(2,1)} %collective-permute-done.1.refs_1_), channel_id=1, source_target_pairs={{0,1},{1,0},{2,3},{3,2},{4,5},{5,4},{6,7},{7,6}} | collective-permute-start | bytes 15925256 | tf_op jit(solution)/shard_map/ppermute | solution.py:260
  621.3 2.5 collective-permute-done.14.refs_0_
  623.9 5.6 collective-permute-start.20
  629.5 0.0 collective-permute-done.5.refs_1_
  629.5 0.0 collective-permute-start.6
  629.5 0.0 collective-permute-done.16.refs_0_
  629.5 1.1 collective-permute-start.18
  630.6 59.1 %collective-permute-done.18.refs_0_ = bf16[1152,1152]{1,0:T(8,128)(2,1)S(1)} collective-permute-done((bf16[1152,1152]{1,0:T(8,128)(2,1)}, bf16[1152,1152]{1,0:T(8,128)(2,1)S(1)}, u32[]{:S(2)}, u32[]{:S(2)}) %collective-permute-start.18) | collective-permute-done | bytes 2654240 | tf_op jit(solution)/shard_map/ppermute | solution.py:260
  689.7 0.0 collective-permute-start.19
  689.7 0.0 collective-permute-done.4.refs_0_
  689.7 0.5 collective-permute-start.17
  690.2 0.0 collective-permute-done.2.refs_2_
  690.2 0.0 collective-permute-start.15
  690.2 9.8 %put.8.refs_4_.refs_2_.refs_3_ = bf16[2,1152,4608]{2,1,0:T(8,128)(2,1)} custom-call(bf16[576,4608]{1,0:T(8,128)(2,1)} %collective-permute-done.refs_0_, bf16[576,4608]{1,0:T(8,128)(2,1)} %collective-permute-done.1.refs_1_, bf16[576,4608]{1,0:T(8,128)(2,1)S(1)} %collective-permute-done.2.refs_2_, ...), custom_call_target="tpu_custom_call", output_to_operand_aliasing={{}: (3, {})} | custom-call | flops 1000000000 | bytes 10000000 | tf_op jit(solution)/shard_map/put/pallas_call | solution.py:246
  700.0 0.0 collective-permute-done.20.refs_0_
  700.0 1.1 collective-permute-start.8
  701.1 0.0 collective-permute-done.6.refs_2_
  701.1 0.2 collective-permute-start.13
  701.3 0.0 copy-start
  701.3 7.0 copy-done
  708.4 2.4 put.10.refs_2_
  710.8 8.2 %put.9.refs_4_ = bf16[2,1152,4608]{2,1,0:T(8,128)(2,1)} custom-call(bf16[576,4608]{1,0:T(8,128)(2,1)S(1)} %collective-permute-done.4.refs_0_, bf16[576,4608]{1,0:T(8,128)(2,1)} %collective-permute-done.5.refs_1_, bf16[576,4608]{1,0:T(8,128)(2,1)S(1)} %collective-permute-done.6.refs_2_, ...), custom_call_target="tpu_custom_call", output_to_operand_aliasing={{}: (3, {})} | custom-call | flops 1000000000 | bytes 10000000 | tf_op jit(solution)/shard_map/put/pallas_call | solution.py:246
  719.0 0.0 collective-permute-done.8.refs_0_
  719.0 0.3 collective-permute-start.11
  719.3 0.0 collective-permute-done.19.refs_1_
  719.3 0.2 collective-permute-start.9
  719.5 0.0 copy-start.1
  719.5 7.0 copy-done.1
  726.6 2.4 put.11.refs_2_
  728.9 0.0 collective-permute-done.17.refs_1_
  729.0 1.5 put.12.refs_2_
  730.5 0.0 collective-permute-done.15.refs_1_
  730.5 2.2 put.13.refs_2_
  732.7 0.0 collective-permute-done.13.refs_1_
  732.7 2.1 put.14.refs_4_
  734.8 0.0 collective-permute-done.11.refs_3_
  734.8 0.0 collective-permute-done.9.refs_1_
  734.8 0.8 put.15
Async XLA Ops:
  116.9 112.1 %collective-permute-start.3 = (bf16[2,288,4608]{2,1,0:T(8,128)(2,1)}, bf16[2,288,4608]{2,1,0:T(8,128)(2,1)}, u32[]{:S(2)}, u32[]{:S(2)}) collective-permute-start(bf16[2,288,4608]{2,1,0:T(8,128)(2,1)} %get-tuple-element.38), channel_id=1, source_target_pairs={{0,2},{1,3},{2,0},{3,1},{4,6},{5,7},{6,4},{7,5}} | collective-permute-start | bytes 15925256 | tf_op jit(solution)/shard_map/ppermute | solution.py:260
  117.6 225.1 %collective-permute-start.7 = (bf16[2,1152,1152]{2,1,0:T(8,128)(2,1)}, bf16[2,1152,1152]{2,1,0:T(8,128)(2,1)}, u32[]{:S(2)}, u32[]{:S(2)}) collective-permute-start(bf16[2,1152,1152]{2,1,0:T(8,128)(2,1)} %get-tuple-element.42), channel_id=1, source_target_pairs={{0,2},{1,3},{2,0},{3,1},{4,6},{5,7},{6,4},{7,5}} | collective-permute-start | bytes 15925256 | tf_op jit(solution)/shard_map/ppermute | solution.py:260
  145.6 310.9 %collective-permute-start.1 = (bf16[576,4608]{1,0:T(8,128)(2,1)}, bf16[576,4608]{1,0:T(8,128)(2,1)}, u32[]{:S(2)}, u32[]{:S(2)}) collective-permute-start(bf16[576,4608]{1,0:T(8,128)(2,1)} %get-tuple-element.35), channel_id=1, source_target_pairs={{0,2},{1,3},{2,0},{3,1},{4,6},{5,7},{6,4},{7,5}} | collective-permute-start | bytes 15925256 | tf_op jit(solution)/shard_map/ppermute | solution.py:260
  146.3 310.9 %collective-permute-start = (bf16[576,4608]{1,0:T(8,128)(2,1)}, bf16[576,4608]{1,0:T(8,128)(2,1)}, u32[]{:S(2)}, u32[]{:S(2)}) collective-permute-start(bf16[576,4608]{1,0:T(8,128)(2,1)} %get-tuple-element.35), channel_id=1, source_target_pairs={{0,1},{1,0},{2,3},{3,2},{4,5},{5,4},{6,7},{7,6}} | collective-permute-start | bytes 15925256 | tf_op jit(solution)/shard_map/ppermute | solution.py:260
  255.0 374.5 %collective-permute-start.5 = (bf16[576,4608]{1,0:T(8,128)(2,1)}, bf16[576,4608]{1,0:T(8,128)(2,1)}, u32[]{:S(2)}, u32[]{:S(2)}) collective-permute-start(bf16[576,4608]{1,0:T(8,128)(2,1)} %get-tuple-element.39), channel_id=1, source_target_pairs={{0,2},{1,3},{2,0},{3,1},{4,6},{5,7},{6,4},{7,5}} | collective-permute-start | bytes 15925256 | tf_op jit(solution)/shard_map/ppermute | solution.py:260
  370.5 259.0 %collective-permute-start.16 = (bf16[576,1152]{1,0:T(8,128)(2,1)}, bf16[576,1152]{1,0:T(8,128)(2,1)S(1)}, u32[]{:S(2)}, u32[]{:S(2)}) collective-permute-start(bf16[576,1152]{1,0:T(8,128)(2,1)} %get-tuple-element.47), channel_id=1, source_target_pairs={{0,2},{1,3},{2,0},{3,1},{4,6},{5,7},{6,4},{7,5}} | collective-permute-start | bytes 3981320 | tf_op jit(solution)/shard_map/ppermute | solution.py:260
  371.2 318.5 %collective-permute-start.4 = (bf16[576,4608]{1,0:T(8,128)(2,1)}, bf16[576,4608]{1,0:T(8,128)(2,1)S(1)}, u32[]{:S(2)}, u32[]{:S(2)}) collective-permute-start(bf16[576,4608]{1,0:T(8,128)(2,1)} %get-tuple-element.39), channel_id=1, source_target_pairs={{0,1},{1,0},{2,3},{3,2},{4,5},{5,4},{6,7},{7,6}} | collective-permute-start | bytes 15925256 | tf_op jit(solution)/shard_map/ppermute | solution.py:260
  456.5 143.7 %collective-permute-start.10 = (bf16[32,1152]{1,0:T(8,128)(2,1)}, bf16[32,1152]{1,0:T(8,128)(2,1)S(1)}, u32[]{:S(2)}, u32[]{:S(2)}) collective-permute-start(bf16[32,1152]{1,0:T(8,128)(2,1)} %get-tuple-element.44), channel_id=1, source_target_pairs={{0,2},{1,3},{2,0},{3,1},{4,6},{5,7},{6,4},{7,5}} | collective-permute-start | bytes 221192 | tf_op jit(solution)/shard_map/ppermute | solution.py:260
  457.2 152.6 %collective-permute-start.12 = (bf16[192,1152]{1,0:T(8,128)(2,1)}, bf16[192,1152]{1,0:T(8,128)(2,1)}, u32[]{:S(2)}, u32[]{:S(2)}) collective-permute-start(bf16[192,1152]{1,0:T(8,128)(2,1)} %get-tuple-element.45), channel_id=1, source_target_pairs={{0,2},{1,3},{2,0},{3,1},{4,6},{5,7},{6,4},{7,5}} | collective-permute-start | bytes 1327112 | tf_op jit(solution)/shard_map/ppermute | solution.py:260
  600.2 23.7 %collective-permute-start.14 = (bf16[288,1152]{1,0:T(8,128)(2,1)}, bf16[288,1152]{1,0:T(8,128)(2,1)S(1)}, u32[]{:S(2)}, u32[]{:S(2)}) collective-permute-start(bf16[288,1152]{1,0:T(8,128)(2,1)} %get-tuple-element.46), channel_id=1, source_target_pairs={{0,2},{1,3},{2,0},{3,1},{4,6},{5,7},{6,4},{7,5}} | collective-permute-start | bytes 1990664 | tf_op jit(solution)/shard_map/ppermute | solution.py:260
  609.7 80.4 %collective-permute-start.2 = (bf16[576,4608]{1,0:T(8,128)(2,1)}, bf16[576,4608]{1,0:T(8,128)(2,1)S(1)}, u32[]{:S(2)}, u32[]{:S(2)}) collective-permute-start(bf16[576,4608]{1,0:T(8,128)(2,1)} %collective-permute-done.1.refs_1_), channel_id=1, source_target_pairs={{0,1},{1,0},{2,3},{3,2},{4,5},{5,4},{6,7},{7,6}} | collective-permute-start | bytes 15925256 | tf_op jit(solution)/shard_map/ppermute | solution.py:260
  623.9 76.1 %collective-permute-start.20 = (bf16[2304,1152]{1,0:T(8,128)(2,1)}, bf16[2304,1152]{1,0:T(8,128)(2,1)S(1)}, u32[]{:S(2)}, u32[]{:S(2)}) collective-permute-start(bf16[2304,1152]{1,0:T(8,128)(2,1)} %get-tuple-element.49), channel_id=1, source_target_pairs={{0,1},{1,0},{2,3},{3,2},{4,5},{5,4},{6,7},{7,6}} | collective-permute-start | bytes 15925256 | tf_op jit(solution)/shard_map/ppermute | solution.py:260
  629.5 71.6 %collective-permute-start.6 = (bf16[576,4608]{1,0:T(8,128)(2,1)}, bf16[576,4608]{1,0:T(8,128)(2,1)S(1)}, u32[]{:S(2)}, u32[]{:S(2)}) collective-permute-start(bf16[576,4608]{1,0:T(8,128)(2,1)} %collective-permute-done.5.refs_1_), channel_id=1, source_target_pairs={{0,1},{1,0},{2,3},{3,2},{4,5},{5,4},{6,7},{7,6}} | collective-permute-start | bytes 15925256 | tf_op jit(solution)/shard_map/ppermute | solution.py:260
  629.5 60.2 %collective-permute-start.18 = (bf16[1152,1152]{1,0:T(8,128)(2,1)}, bf16[1152,1152]{1,0:T(8,128)(2,1)S(1)}, u32[]{:S(2)}, u32[]{:S(2)}) collective-permute-start(bf16[1152,1152]{1,0:T(8,128)(2,1)} %get-tuple-element.48), channel_id=1, source_target_pairs={{0,2},{1,3},{2,0},{3,1},{4,6},{5,7},{6,4},{7,5}} | collective-permute-start | bytes 7962632 | tf_op jit(solution)/shard_map/ppermute | solution.py:260
  689.7 29.6 %collective-permute-start.19 = (bf16[1152,1152]{1,0:T(8,128)(2,1)S(1)}, bf16[1152,1152]{1,0:T(8,128)(2,1)S(1)}, u32[]{:S(2)}, u32[]{:S(2)}) collective-permute-start(bf16[1152,1152]{1,0:T(8,128)(2,1)S(1)} %collective-permute-done.18.refs_0_), channel_id=1, source_target_pairs={{0,1},{1,0},{2,3},{3,2},{4,5},{5,4},{6,7},{7,6}} | collective-permute-start | bytes 7962632 | tf_op jit(solution)/shard_map/ppermute | solution.py:260
  689.7 39.3 %collective-permute-start.17 = (bf16[576,1152]{1,0:T(8,128)(2,1)S(1)}, bf16[576,1152]{1,0:T(8,128)(2,1)S(1)}, u32[]{:S(2)}, u32[]{:S(2)}) collective-permute-start(bf16[576,1152]{1,0:T(8,128)(2,1)S(1)} %collective-permute-done.16.refs_0_), channel_id=1, source_target_pairs={{0,1},{1,0},{2,3},{3,2},{4,5},{5,4},{6,7},{7,6}} | collective-permute-start | bytes 3981320 | tf_op jit(solution)/shard_map/ppermute | solution.py:260
  690.2 40.3 %collective-permute-start.15 = (bf16[288,1152]{1,0:T(8,128)(2,1)S(1)}, bf16[288,1152]{1,0:T(8,128)(2,1)}, u32[]{:S(2)}, u32[]{:S(2)}) collective-permute-start(bf16[288,1152]{1,0:T(8,128)(2,1)S(1)} %collective-permute-done.14.refs_0_), channel_id=1, source_target_pairs={{0,1},{1,0},{2,3},{3,2},{4,5},{5,4},{6,7},{7,6}} | collective-permute-start | bytes 1990664 | tf_op jit(solution)/shard_map/ppermute | solution.py:260
  700.0 19.0 %collective-permute-start.8 = (bf16[64,1152]{1,0:T(8,128)(2,1)}, bf16[64,1152]{1,0:T(8,128)(2,1)S(1)}, u32[]{:S(2)}, u32[]{:S(2)}) collective-permute-start(bf16[64,1152]{1,0:T(8,128)(2,1)} %get-tuple-element.43), channel_id=1, source_target_pairs={{0,2},{1,3},{2,0},{3,1},{4,6},{5,7},{6,4},{7,5}} | collective-permute-start | bytes 442376 | tf_op jit(solution)/shard_map/ppermute | solution.py:260
  701.1 31.6 %collective-permute-start.13 = (bf16[192,1152]{1,0:T(8,128)(2,1)}, bf16[192,1152]{1,0:T(8,128)(2,1)}, u32[]{:S(2)}, u32[]{:S(2)}) collective-permute-start(bf16[192,1152]{1,0:T(8,128)(2,1)} %collective-permute-done.12.refs_0_), channel_id=1, source_target_pairs={{0,1},{1,0},{2,3},{3,2},{4,5},{5,4},{6,7},{7,6}} | collective-permute-start | bytes 1327112 | tf_op jit(solution)/shard_map/ppermute | solution.py:260
  701.3 7.0 copy-start
  719.0 15.8 %collective-permute-start.11 = (bf16[32,1152]{1,0:T(8,128)(2,1)S(1)}, bf16[32,1152]{1,0:T(8,128)(2,1)S(1)}, u32[]{:S(2)}, u32[]{:S(2)}) collective-permute-start(bf16[32,1152]{1,0:T(8,128)(2,1)S(1)} %collective-permute-done.10.refs_2_), channel_id=1, source_target_pairs={{0,1},{1,0},{2,3},{3,2},{4,5},{5,4},{6,7},{7,6}} | collective-permute-start | bytes 221192 | tf_op jit(solution)/shard_map/ppermute | solution.py:260
  719.3 15.5 %collective-permute-start.9 = (bf16[64,1152]{1,0:T(8,128)(2,1)S(1)}, bf16[64,1152]{1,0:T(8,128)(2,1)S(1)}, u32[]{:S(2)}, u32[]{:S(2)}) collective-permute-start(bf16[64,1152]{1,0:T(8,128)(2,1)S(1)} %collective-permute-done.8.refs_0_), channel_id=1, source_target_pairs={{0,1},{1,0},{2,3},{3,2},{4,5},{5,4},{6,7},{7,6}} | collective-permute-start | bytes 442376 | tf_op jit(solution)/shard_map/ppermute | solution.py:260
  719.5 7.0 copy-start.1

commit v5 on v4

--- a/solution.py
+++ b/solution.py
@@ -260,7 +260,7 @@
     return lax.ppermute(array, "dp", pairs)
 
 
-LAST = (1152, 576, 288, 192, 64, 32)
+LAST = (1152, 576, 368, 144, 48, 16)
 
 
 def solution(mesh):
@@ -289,8 +289,8 @@
                 over = [send(a, ACROSS) for a in parts]
                 passed = [send(a, PARTNER) for a in over]
                 for i in range(5):
-                    last = (4, 5) if i == 4 else (i,)
-                    pairs = [(which, splits[1 + j][0], a[j]) for j in last for which, a in ((2, over), (3, passed))]
+                    here, handed = ((i, i + 1, i + 2), (i,)) if i == 3 else ((), (4, 5)) if i == 4 else ((i,), (i,))
+                    pairs = [(2, splits[1 + j][0], over[j]) for j in here] + [(3, splits[1 + j][0], passed[j]) for j in handed]
                     w = put(w, block, pairs, new_w if i == 0 else ())
             new_w.append(w)
             new_m.append(m)

time: 736 us -> 738 us (level)
  waiting for transfers between devices: 448 us -> 462 us
  starting transfers between devices: 46.6 us -> 35.4 us
    ppermute x21, waiting for transfers between devices: 448 us -> 462 us  [send(): return lax.ppermute(array, 'dp', pairs)]
    ppermute x21, starting transfers between devices: 46.6 us -> 35.4 us  [send(): return lax.ppermute(array, 'dp', pairs)]
  transfers between devices with their start and end apart: 21 -> 21, of which waited for: 7 -> 6; matrix products, arithmetic and copies ran while one was open for 0% -> 0% of each run, Pallas kernels for 15% -> 15%
where the time goes in v5:
time: 738 us
  waiting for transfers between devices  462 us (63%)
  Pallas kernels  225 us (30%)
  starting transfers between devices  35.4 us (5%)
  local copies, waits for them, and re-layouts  14.1 us (2%)
    ppermute x21, waiting for transfers between devices, send(): return lax.ppermute(array, 'dp', pairs)  462 us
    pallas_call x1, Pallas kernels, exchange(): pl.pallas_call(pair_sums, out_shape=[jax.ShapeDtypeStruct(s, BF16) for s...  116 us
    pallas_call x3, Pallas kernels, adamw(): pl.pallas_call(body, grid_spec=pltpu.PrefetchScalarGridSpec(num_scalar_pr...  79.5 us
    ppermute x21, starting transfers between devices, send(): return lax.ppermute(array, 'dp', pairs)  35.4 us
    pallas_call x8, Pallas kernels, put(): pl.pallas_call(body, in_specs=[*(pl.BlockSpec(memory_space=pltpu.VMEM) fo...  29.2 us
  transfers between devices with their start and end apart: 21, of which 6 were waited for; matrix products, arithmetic and copies ran while one was open for 0% of the time, Pallas kernels for 15%

profile of v5, /device:TPU:0, one launch (start us, length us, event | category | flops | bytes accessed | tf_op | source)
XLA Modules:
  0.0 738.1 jit_solution(8485609721133717644)
XLA Ops:
  0.6 116.2 %pair_sums.1 = (bf16[2,288,4608]{2,1,0:T(8,128)(2,1)}, bf16[2,288,4608]{2,1,0:T(8,128)(2,1)}, bf16[2,288,4608]{2,1,0:T(8,128)(2,1)}, bf16[2,1152,1152]{2,1,0:T(8...) custom-call(bf16[1,2,1152,4608]{3,2,1,0:T(8,128)(2,1)} %g_ref.3, ...), custom_call_target="tpu_custom_call" | custom-call | flops 100000000 | bytes 100000000 | tf_op jit(solution)/shard_map/pair_sums/pallas_call | solution.py:131
  116.9 0.7 collective-permute-start.3
  117.6 1.3 collective-permute-start.7
  118.9 0.5 iota_xor_fusion.where_ref
  119.5 26.0 %adamw.3 = (f32[2,288,4608]{2,1,0:T(8,128)}, f32[2,288,4608]{2,1,0:T(8,128)}, bf16[2,1152,4608]{2,1,0:T(8,128)(2,1)}, bf16[576,4608]{1,0:T(8,128)(2,1)}) custom-call(s32[4]{0:T(128)} %iota_xor_fusion.where_ref, bf16[1,2,1152,4608]{3,2,1,0:T(8,128)(2,1)} %g_ref.3, bf16[2,288,4608]{2,1,0:T(8,128)(2,1)} %get-tuple-element.33.theirs_ref, ...), custom_call_target="tpu_custom_call" | custom-call | flops 10000000000 | bytes 100000000 | tf_op jit(solution)/shard_map/adamw/pallas_call | solution.py:191
  145.5 0.7 collective-permute-start.1
  146.2 6.9 collective-permute-start
  153.0 75.9 %collective-permute-done.3.arrived_ref = bf16[2,288,4608]{2,1,0:T(8,128)(2,1)} collective-permute-done((bf16[2,288,4608]{2,1,0:T(8,128)(2,1)}, bf16[2,288,4608]{2,1,0:T(8,128)(2,1)}, u32[]{:S(2)}, u32[]{:S(2)}) %collective-permute-start.3) | collective-permute-done | bytes 5308448 | tf_op jit(solution)/shard_map/ppermute | solution.py:260
  229.0 25.9 %adamw.4 = (f32[2,288,4608]{2,1,0:T(8,128)}, f32[2,288,4608]{2,1,0:T(8,128)}, bf16[2,1152,4608]{2,1,0:T(8,128)(2,1)}, bf16[576,4608]{1,0:T(8,128)(2,1)}) custom-call(s32[4]{0:T(128)} %iota_xor_fusion.where_ref, bf16[1,2,1152,4608]{3,2,1,0:T(8,128)(2,1)} %g_ref.4, bf16[2,288,4608]{2,1,0:T(8,128)(2,1)} %get-tuple-element.37.theirs_ref, ...), custom_call_target="tpu_custom_call" | custom-call | flops 10000000000 | bytes 100000000 | tf_op jit(solution)/shard_map/adamw/pallas_call | solution.py:191
  254.9 0.7 collective-permute-start.5
  255.6 87.1 %collective-permute-done.7.arrived_ref = bf16[2,1152,1152]{2,1,0:T(8,128)(2,1)} collective-permute-done((bf16[2,1152,1152]{2,1,0:T(8,128)(2,1)}, bf16[2,1152,1152]{2,1,0:T(8,128)(2,1)}, u32[]{:S(2)}, u32[]{:S(2)}) %collective-permute-start.7) | collective-permute-done | bytes 5308448 | tf_op jit(solution)/shard_map/ppermute | solution.py:260
  342.7 27.6 %adamw.5 = (f32[2,1152,1152]{2,1,0:T(8,128)}, f32[2,1152,1152]{2,1,0:T(8,128)}, bf16[2,4608,1152]{2,1,0:T(8,128)(2,1)}, bf16[2304,1152]{1,0:T(8,128)(2,1)}, bf16...) custom-call(s32[4]{0:T(128)} %iota_xor_fusion.where_ref, ...), custom_call_target="tpu_custom_call" | custom-call | flops 10000000000 | bytes 100000000 | tf_op jit(solution)/shard_map/adamw/pallas_call | solution.py:191
  370.4 0.7 collective-permute-start.16
  371.1 12.2 %collective-permute-start.4 = (bf16[576,4608]{1,0:T(8,128)(2,1)}, bf16[576,4608]{1,0:T(8,128)(2,1)S(1)}, u32[]{:S(2)}, u32[]{:S(2)}) collective-permute-start(bf16[576,4608]{1,0:T(8,128)(2,1)} %get-tuple-element.39), channel_id=1, source_target_pairs={{0,1},{1,0},{2,3},{3,2},{4,5},{5,4},{6,7},{7,6}} | collective-permute-start | bytes 15925256 | tf_op jit(solution)/shard_map/ppermute | solution.py:260
  383.2 73.2 %collective-permute-done.1.refs_1_ = bf16[576,4608]{1,0:T(8,128)(2,1)} collective-permute-done((bf16[576,4608]{1,0:T(8,128)(2,1)}, bf16[576,4608]{1,0:T(8,128)(2,1)}, u32[]{:S(2)}, u32[]{:S(2)}) %collective-permute-start.1) | collective-permute-done | bytes 5308448 | tf_op jit(solution)/shard_map/ppermute | solution.py:260
  456.5 0.7 collective-permute-start.14
  457.2 0.0 collective-permute-done.refs_0_
  457.2 1.3 collective-permute-start.10
  458.5 159.0 %collective-permute-done.10.refs_2_ = bf16[16,1152]{1,0:T(8,128)(2,1)S(1)} collective-permute-done((bf16[16,1152]{1,0:T(8,128)(2,1)}, bf16[16,1152]{1,0:T(8,128)(2,1)S(1)}, u32[]{:S(2)}, u32[]{:S(2)}) %collective-permute-start.10) | collective-permute-done | bytes 36896 | tf_op jit(solution)/shard_map/ppermute | solution.py:260
  617.5 0.7 collective-permute-start.12
  618.2 8.6 %collective-permute-done.12.refs_0_ = bf16[144,1152]{1,0:T(8,128)(2,1)S(1)} collective-permute-done((bf16[144,1152]{1,0:T(8,128)(2,1)}, bf16[144,1152]{1,0:T(8,128)(2,1)S(1)}, u32[]{:S(2)}, u32[]{:S(2)}) %collective-permute-start.12) | collective-permute-done | bytes 331808 | tf_op jit(solution)/shard_map/ppermute | solution.py:260
  626.9 0.0 copy-start.2
  626.9 4.7 collective-permute-start.2
  631.6 0.0 collective-permute-done.14.refs_0_
  631.6 0.0 collective-permute-start.20
  631.7 0.0 collective-permute-done.5.refs_1_
  631.7 0.5 collective-permute-start.6
  632.1 0.0 collective-permute-done.16.refs_0_
  632.2 1.5 collective-permute-start.18
  633.6 58.3 %collective-permute-done.18.refs_0_ = bf16[1152,1152]{1,0:T(8,128)(2,1)S(1)} collective-permute-done((bf16[1152,1152]{1,0:T(8,128)(2,1)}, bf16[1152,1152]{1,0:T(8,128)(2,1)S(1)}, u32[]{:S(2)}, u32[]{:S(2)}) %collective-permute-start.18) | collective-permute-done | bytes 2654240 | tf_op jit(solution)/shard_map/ppermute | solution.py:260
  691.9 0.0 collective-permute-start.19
  691.9 0.0 collective-permute-done.4.refs_0_
  691.9 0.5 collective-permute-start.17
  692.4 0.0 collective-permute-done.2.refs_2_
  692.4 0.0 copy-done.2
  692.4 0.0 collective-permute-start.15
  692.4 9.8 %put.8.refs_4_.refs_2_.refs_3_ = bf16[2,1152,4608]{2,1,0:T(8,128)(2,1)} custom-call(bf16[576,4608]{1,0:T(8,128)(2,1)} %collective-permute-done.refs_0_, bf16[576,4608]{1,0:T(8,128)(2,1)} %collective-permute-done.1.refs_1_, bf16[576,4608]{1,0:T(8,128)(2,1)S(1)} %collective-permute-done.2.refs_2_, ...), custom_call_target="tpu_custom_call", output_to_operand_aliasing={{}: (3, {})} | custom-call | flops 1000000000 | bytes 10000000 | tf_op jit(solution)/shard_map/put/pallas_call | solution.py:246
  702.2 0.0 collective-permute-done.20.refs_0_
  702.2 1.5 collective-permute-start.8
  703.7 0.0 copy-start
  703.7 7.0 copy-done
  710.7 2.4 put.10.refs_2_
  713.1 0.0 collective-permute-done.6.refs_2_
  713.1 0.2 collective-permute-start.13
  713.4 8.2 %put.9.refs_4_ = bf16[2,1152,4608]{2,1,0:T(8,128)(2,1)} custom-call(bf16[576,4608]{1,0:T(8,128)(2,1)S(1)} %collective-permute-done.4.refs_0_, bf16[576,4608]{1,0:T(8,128)(2,1)} %collective-permute-done.5.refs_1_, bf16[576,4608]{1,0:T(8,128)(2,1)S(1)} %collective-permute-done.6.refs_2_, ...), custom_call_target="tpu_custom_call", output_to_operand_aliasing={{}: (3, {})} | custom-call | flops 1000000000 | bytes 10000000 | tf_op jit(solution)/shard_map/put/pallas_call | solution.py:246
  721.6 0.0 collective-permute-done.8.refs_1_
  721.6 0.3 collective-permute-start.11
  721.9 0.0 collective-permute-done.19.refs_1_
  721.9 0.2 collective-permute-start.9
  722.1 0.0 copy-start.1
  722.1 7.0 copy-done.1
  729.1 2.4 put.11.refs_2_
  731.5 0.0 collective-permute-done.17.refs_1_
  731.6 1.5 put.12.refs_2_
  733.1 0.0 copy-start.3
  733.1 0.0 collective-permute-done.15.refs_1_
  733.1 2.4 put.13.refs_4_
  735.5 0.0 collective-permute-done.13.refs_3_
  735.5 0.0 copy-done.3
  735.5 1.8 put.14.refs_2_
  737.4 0.0 collective-permute-done.11.refs_1_
  737.4 0.0 collective-permute-done.9.refs_0_
  737.4 0.7 put.15
Async XLA Ops:
  116.9 112.1 %collective-permute-start.3 = (bf16[2,288,4608]{2,1,0:T(8,128)(2,1)}, bf16[2,288,4608]{2,1,0:T(8,128)(2,1)}, u32[]{:S(2)}, u32[]{:S(2)}) collective-permute-start(bf16[2,288,4608]{2,1,0:T(8,128)(2,1)} %get-tuple-element.38), channel_id=1, source_target_pairs={{0,2},{1,3},{2,0},{3,1},{4,6},{5,7},{6,4},{7,5}} | collective-permute-start | bytes 15925256 | tf_op jit(solution)/shard_map/ppermute | solution.py:260
  117.6 225.1 %collective-permute-start.7 = (bf16[2,1152,1152]{2,1,0:T(8,128)(2,1)}, bf16[2,1152,1152]{2,1,0:T(8,128)(2,1)}, u32[]{:S(2)}, u32[]{:S(2)}) collective-permute-start(bf16[2,1152,1152]{2,1,0:T(8,128)(2,1)} %get-tuple-element.42), channel_id=1, source_target_pairs={{0,2},{1,3},{2,0},{3,1},{4,6},{5,7},{6,4},{7,5}} | collective-permute-start | bytes 15925256 | tf_op jit(solution)/shard_map/ppermute | solution.py:260
  145.5 311.0 %collective-permute-start.1 = (bf16[576,4608]{1,0:T(8,128)(2,1)}, bf16[576,4608]{1,0:T(8,128)(2,1)}, u32[]{:S(2)}, u32[]{:S(2)}) collective-permute-start(bf16[576,4608]{1,0:T(8,128)(2,1)} %get-tuple-element.35), channel_id=1, source_target_pairs={{0,2},{1,3},{2,0},{3,1},{4,6},{5,7},{6,4},{7,5}} | collective-permute-start | bytes 15925256 | tf_op jit(solution)/shard_map/ppermute | solution.py:260
  146.2 311.0 %collective-permute-start = (bf16[576,4608]{1,0:T(8,128)(2,1)}, bf16[576,4608]{1,0:T(8,128)(2,1)}, u32[]{:S(2)}, u32[]{:S(2)}) collective-permute-start(bf16[576,4608]{1,0:T(8,128)(2,1)} %get-tuple-element.35), channel_id=1, source_target_pairs={{0,1},{1,0},{2,3},{3,2},{4,5},{5,4},{6,7},{7,6}} | collective-permute-start | bytes 15925256 | tf_op jit(solution)/shard_map/ppermute | solution.py:260
  254.9 376.8 %collective-permute-start.5 = (bf16[576,4608]{1,0:T(8,128)(2,1)}, bf16[576,4608]{1,0:T(8,128)(2,1)}, u32[]{:S(2)}, u32[]{:S(2)}) collective-permute-start(bf16[576,4608]{1,0:T(8,128)(2,1)} %get-tuple-element.39), channel_id=1, source_target_pairs={{0,2},{1,3},{2,0},{3,1},{4,6},{5,7},{6,4},{7,5}} | collective-permute-start | bytes 15925256 | tf_op jit(solution)/shard_map/ppermute | solution.py:260
  370.4 261.8 %collective-permute-start.16 = (bf16[576,1152]{1,0:T(8,128)(2,1)}, bf16[576,1152]{1,0:T(8,128)(2,1)S(1)}, u32[]{:S(2)}, u32[]{:S(2)}) collective-permute-start(bf16[576,1152]{1,0:T(8,128)(2,1)} %get-tuple-element.47), channel_id=1, source_target_pairs={{0,2},{1,3},{2,0},{3,1},{4,6},{5,7},{6,4},{7,5}} | collective-permute-start | bytes 3981320 | tf_op jit(solution)/shard_map/ppermute | solution.py:260
  371.1 320.8 %collective-permute-start.4 = (bf16[576,4608]{1,0:T(8,128)(2,1)}, bf16[576,4608]{1,0:T(8,128)(2,1)S(1)}, u32[]{:S(2)}, u32[]{:S(2)}) collective-permute-start(bf16[576,4608]{1,0:T(8,128)(2,1)} %get-tuple-element.39), channel_id=1, source_target_pairs={{0,1},{1,0},{2,3},{3,2},{4,5},{5,4},{6,7},{7,6}} | collective-permute-start | bytes 15925256 | tf_op jit(solution)/shard_map/ppermute | solution.py:260
  456.5 175.1 %collective-permute-start.14 = (bf16[368,1152]{1,0:T(8,128)(2,1)}, bf16[368,1152]{1,0:T(8,128)(2,1)S(1)}, u32[]{:S(2)}, u32[]{:S(2)}) collective-permute-start(bf16[368,1152]{1,0:T(8,128)(2,1)} %get-tuple-element.46), channel_id=1, source_target_pairs={{0,2},{1,3},{2,0},{3,1},{4,6},{5,7},{6,4},{7,5}} | collective-permute-start | bytes 2543624 | tf_op jit(solution)/shard_map/ppermute | solution.py:260
  457.2 160.4 %collective-permute-start.10 = (bf16[16,1152]{1,0:T(8,128)(2,1)}, bf16[16,1152]{1,0:T(8,128)(2,1)S(1)}, u32[]{:S(2)}, u32[]{:S(2)}) collective-permute-start(bf16[16,1152]{1,0:T(8,128)(2,1)} %get-tuple-element.44), channel_id=1, source_target_pairs={{0,2},{1,3},{2,0},{3,1},{4,6},{5,7},{6,4},{7,5}} | collective-permute-start | bytes 110600 | tf_op jit(solution)/shard_map/ppermute | solution.py:260
  617.5 9.3 %collective-permute-start.12 = (bf16[144,1152]{1,0:T(8,128)(2,1)}, bf16[144,1152]{1,0:T(8,128)(2,1)S(1)}, u32[]{:S(2)}, u32[]{:S(2)}) collective-permute-start(bf16[144,1152]{1,0:T(8,128)(2,1)} %get-tuple-element.45), channel_id=1, source_target_pairs={{0,2},{1,3},{2,0},{3,1},{4,6},{5,7},{6,4},{7,5}} | collective-permute-start | bytes 995336 | tf_op jit(solution)/shard_map/ppermute | solution.py:260
  626.9 65.5 %copy-start.2 = (bf16[144,1152]{1,0:T(8,128)(2,1)}, bf16[144,1152]{1,0:T(8,128)(2,1)S(1)}, u32[]{:S(2)}) copy-start(bf16[144,1152]{1,0:T(8,128)(2,1)S(1)} %collective-permute-done.12.refs_0_) | copy-start | bytes 995332
  626.9 65.5 %collective-permute-start.2 = (bf16[576,4608]{1,0:T(8,128)(2,1)}, bf16[576,4608]{1,0:T(8,128)(2,1)S(1)}, u32[]{:S(2)}, u32[]{:S(2)}) collective-permute-start(bf16[576,4608]{1,0:T(8,128)(2,1)} %collective-permute-done.1.refs_1_), channel_id=1, source_target_pairs={{0,1},{1,0},{2,3},{3,2},{4,5},{5,4},{6,7},{7,6}} | collective-permute-start | bytes 15925256 | tf_op jit(solution)/shard_map/ppermute | solution.py:260
  631.6 70.6 %collective-permute-start.20 = (bf16[2304,1152]{1,0:T(8,128)(2,1)}, bf16[2304,1152]{1,0:T(8,128)(2,1)S(1)}, u32[]{:S(2)}, u32[]{:S(2)}) collective-permute-start(bf16[2304,1152]{1,0:T(8,128)(2,1)} %get-tuple-element.49), channel_id=1, source_target_pairs={{0,1},{1,0},{2,3},{3,2},{4,5},{5,4},{6,7},{7,6}} | collective-permute-start | bytes 15925256 | tf_op jit(solution)/shard_map/ppermute | solution.py:260
  631.7 81.5 %collective-permute-start.6 = (bf16[576,4608]{1,0:T(8,128)(2,1)}, bf16[576,4608]{1,0:T(8,128)(2,1)S(1)}, u32[]{:S(2)}, u32[]{:S(2)}) collective-permute-start(bf16[576,4608]{1,0:T(8,128)(2,1)} %collective-permute-done.5.refs_1_), channel_id=1, source_target_pairs={{0,1},{1,0},{2,3},{3,2},{4,5},{5,4},{6,7},{7,6}} | collective-permute-start | bytes 15925256 | tf_op jit(solution)/shard_map/ppermute | solution.py:260
  632.2 59.7 %collective-permute-start.18 = (bf16[1152,1152]{1,0:T(8,128)(2,1)}, bf16[1152,1152]{1,0:T(8,128)(2,1)S(1)}, u32[]{:S(2)}, u32[]{:S(2)}) collective-permute-start(bf16[1152,1152]{1,0:T(8,128)(2,1)} %get-tuple-element.48), channel_id=1, source_target_pairs={{0,2},{1,3},{2,0},{3,1},{4,6},{5,7},{6,4},{7,5}} | collective-permute-start | bytes 7962632 | tf_op jit(solution)/shard_map/ppermute | solution.py:260
  691.9 30.1 %collective-permute-start.19 = (bf16[1152,1152]{1,0:T(8,128)(2,1)S(1)}, bf16[1152,1152]{1,0:T(8,128)(2,1)S(1)}, u32[]{:S(2)}, u32[]{:S(2)}) collective-permute-start(bf16[1152,1152]{1,0:T(8,128)(2,1)S(1)} %collective-permute-done.18.refs_0_), channel_id=1, source_target_pairs={{0,1},{1,0},{2,3},{3,2},{4,5},{5,4},{6,7},{7,6}} | collective-permute-start | bytes 7962632 | tf_op jit(solution)/shard_map/ppermute | solution.py:260
  691.9 39.7 %collective-permute-start.17 = (bf16[576,1152]{1,0:T(8,128)(2,1)S(1)}, bf16[576,1152]{1,0:T(8,128)(2,1)S(1)}, u32[]{:S(2)}, u32[]{:S(2)}) collective-permute-start(bf16[576,1152]{1,0:T(8,128)(2,1)S(1)} %collective-permute-done.16.refs_0_), channel_id=1, source_target_pairs={{0,1},{1,0},{2,3},{3,2},{4,5},{5,4},{6,7},{7,6}} | collective-permute-start | bytes 3981320 | tf_op jit(solution)/shard_map/ppermute | solution.py:260
  692.4 40.7 %collective-permute-start.15 = (bf16[368,1152]{1,0:T(8,128)(2,1)S(1)}, bf16[368,1152]{1,0:T(8,128)(2,1)}, u32[]{:S(2)}, u32[]{:S(2)}) collective-permute-start(bf16[368,1152]{1,0:T(8,128)(2,1)S(1)} %collective-permute-done.14.refs_0_), channel_id=1, source_target_pairs={{0,1},{1,0},{2,3},{3,2},{4,5},{5,4},{6,7},{7,6}} | collective-permute-start | bytes 2543624 | tf_op jit(solution)/shard_map/ppermute | solution.py:260
  702.2 19.3 %collective-permute-start.8 = (bf16[48,1152]{1,0:T(8,128)(2,1)}, bf16[48,1152]{1,0:T(8,128)(2,1)}, u32[]{:S(2)}, u32[]{:S(2)}) collective-permute-start(bf16[48,1152]{1,0:T(8,128)(2,1)} %get-tuple-element.43), channel_id=1, source_target_pairs={{0,2},{1,3},{2,0},{3,1},{4,6},{5,7},{6,4},{7,5}} | collective-permute-start | bytes 331784 | tf_op jit(solution)/shard_map/ppermute | solution.py:260
  703.7 7.0 copy-start
  713.1 22.4 %collective-permute-start.13 = (bf16[144,1152]{1,0:T(8,128)(2,1)}, bf16[144,1152]{1,0:T(8,128)(2,1)S(1)}, u32[]{:S(2)}, u32[]{:S(2)}) collective-permute-start(bf16[144,1152]{1,0:T(8,128)(2,1)} %copy-done.2), channel_id=1, source_target_pairs={{0,1},{1,0},{2,3},{3,2},{4,5},{5,4},{6,7},{7,6}} | collective-permute-start | bytes 995336 | tf_op jit(solution)/shard_map/ppermute | solution.py:260
  721.6 15.8 %collective-permute-start.11 = (bf16[16,1152]{1,0:T(8,128)(2,1)S(1)}, bf16[16,1152]{1,0:T(8,128)(2,1)S(1)}, u32[]{:S(2)}, u32[]{:S(2)}) collective-permute-start(bf16[16,1152]{1,0:T(8,128)(2,1)S(1)} %collective-permute-done.10.refs_2_), channel_id=1, source_target_pairs={{0,1},{1,0},{2,3},{3,2},{4,5},{5,4},{6,7},{7,6}} | collective-permute-start | bytes 110600 | tf_op jit(solution)/shard_map/ppermute | solution.py:260
  721.9 15.5 %collective-permute-start.9 = (bf16[48,1152]{1,0:T(8,128)(2,1)}, bf16[48,1152]{1,0:T(8,128)(2,1)S(1)}, u32[]{:S(2)}, u32[]{:S(2)}) collective-permute-start(bf16[48,1152]{1,0:T(8,128)(2,1)} %collective-permute-done.8.refs_1_), channel_id=1, source_target_pairs={{0,1},{1,0},{2,3},{3,2},{4,5},{5,4},{6,7},{7,6}} | collective-permute-start | bytes 331784 | tf_op jit(solution)/shard_map/ppermute | solution.py:260
  722.1 7.0 copy-start.1
  733.1 2.4 copy-start.3
